TPU v7x, 16 devices: a 4x2x1 block of a 4x4x8 slice. The times are simulated.
16 devices in a mesh: dp: 2 (over y, z), sp: 8 (over x, core).
Axes of the slice: x: 4, y: 2, z: 1, core: 2. Of those that a mesh axis runs over, the one named last changes fastest.
The devices are a block of a 4x4x8 slice.
Arguments:
- x_in: bfloat16 [12, 1024, 1024], P('dp', 'sp'), parts along dimension 0
- positions: int32 [2048], P(('dp', 'sp')), parts along dimension 0
- d_out: bfloat16 [12, 1024, 1024], P('dp', 'sp'), parts along dimension 0
- w_query: bfloat16 [2, 1024, 16, 64], replicated
- w_key: bfloat16 [2, 1024, 16, 64], replicated
- w_value: bfloat16 [2, 1024, 16, 64], replicated
- w_attn_out: bfloat16 [2, 16, 64, 1024], replicated
- w_up: bfloat16 [2, 1024, 4096], replicated
- w_down: bfloat16 [2, 4096, 1024], replicated
- g_attn: float32 [2, 1024], replicated
- g_mlp: float32 [2, 1024], replicated
- learn_rate: float32 [], replicated
Outputs:
- output 1: bfloat16 [12, 1024, 1024], P('dp', 'sp'), parts along dimension 0
- output 2: bfloat16 [12, 1024, 1024], P('dp', 'sp'), parts along dimension 0
- output 3: bfloat16 [4, 1024, 16, 64], P('dp'), parts along dimension 0
- output 4: bfloat16 [4, 1024, 16, 64], P('dp'), parts along dimension 0
- output 5: bfloat16 [4, 1024, 16, 64], P('dp'), parts along dimension 0
- output 6: bfloat16 [4, 16, 64, 1024], P('dp'), parts along dimension 0
- output 7: bfloat16 [4, 1024, 4096], P('dp'), parts along dimension 0
- output 8: bfloat16 [4, 4096, 1024], P('dp'), parts along dimension 0
There are 2 independent parts. A program takes and returns all parts, laid end to end along the dimension named above; an argument that names none is the same for every part.
All inputs are finite; a program needn't handle non-finite values.
Results may differ from a plain program's by a relative error of at most 0.02.
Values are sent between devices in bfloat16 or wider.
A program may use at most 768 MiB of HBM per device.

v0:
```python
import jax
import jax.numpy as jnp
from jax import lax
from jax.sharding import PartitionSpec as P

EPSILON = 1e-5
ROPE_BASE = 10000.0
SEQ_AXIS = 'sp'


def contract(form, left, right):
    return jnp.einsum(form, left, right, preferred_element_type=jnp.float32)


def gelu_tanh(value):
    return jax.nn.gelu(value, approximate=True)


def rms_norm(act, gain):
    wide = act.astype(jnp.float32)
    inv_rms = lax.rsqrt(jnp.mean(wide * wide, axis=-1, keepdims=True) + EPSILON)
    return (wide * inv_rms * gain).astype(jnp.bfloat16), inv_rms


def rms_norm_grad(act, inv_rms, gain, d_norm):
    wide = act.astype(jnp.float32)
    d_gain = d_norm * gain
    return inv_rms * d_gain - wide * inv_rms ** 3 * jnp.mean(d_gain * wide, axis=-1, keepdims=True)


def rotary(heads, positions, sign):
    half_dim = heads.shape[-1] // 2
    inv_freq = ROPE_BASE ** (-2.0 * jnp.arange(half_dim, dtype=jnp.float32) / heads.shape[-1])
    angle = positions.astype(jnp.float32)[..., None] * inv_freq
    cosine = jnp.cos(angle)[..., None, :]
    sine = sign * jnp.sin(angle)[..., None, :]
    first = heads[..., :half_dim]
    second = heads[..., half_dim:]
    return jnp.concatenate([first * cosine - second * sine, second * cosine + first * sine], axis=-1)


def causal_scores(q_heads, k_heads):
    scores = contract('bqgre,bkge->bgrqk', q_heads, k_heads) * q_heads.shape[-1] ** -0.5
    allowed = jnp.arange(q_heads.shape[1])[:, None] >= jnp.arange(k_heads.shape[1])[None, :]
    return jnp.where(allowed, scores, -1e30)


def attn_forward(q_heads, k_heads, v_heads):
    scores = causal_scores(q_heads, k_heads)
    row_max = jnp.max(scores, axis=-1, keepdims=True)
    shifted_exp = jnp.exp(scores - row_max)
    row_sum = jnp.sum(shifted_exp, axis=-1, keepdims=True)
    probs_low = (shifted_exp / row_sum).astype(jnp.bfloat16)
    attn_out = contract('bgrqk,bkge->bqgre', probs_low, v_heads).astype(jnp.bfloat16)
    return attn_out, (row_max + jnp.log(row_sum))[..., 0]


def attn_backward(q_heads, k_heads, v_heads, out_heads, log_sum, d_heads):
    probs = jnp.exp(causal_scores(q_heads, k_heads) - log_sum[..., None])
    probs_low = probs.astype(jnp.bfloat16)
    d_values = contract('bgrqk,bqgre->bkge', probs_low, d_heads)
    d_probs = contract('bqgre,bkge->bgrqk', d_heads, v_heads)
    delta = contract('bqgre,bqgre->bgrq', d_heads, out_heads)
    d_scores = (probs * (d_probs - delta[..., None]) * q_heads.shape[-1] ** -0.5).astype(jnp.bfloat16)
    d_query = contract('bgrqk,bkge->bqgre', d_scores, k_heads)
    d_keys = contract('bgrqk,bqgre->bkge', d_scores, q_heads)
    return d_query, d_keys, d_values


def to_heads(tensor):
    return lax.all_to_all(tensor, SEQ_AXIS, 2, 1, tiled=True)


def to_seq(tensor):
    return lax.all_to_all(tensor, SEQ_AXIS, 1, 2, tiled=True)


def solution(mesh):
    act_spec = P('dp', 'sp', None)
    pos_spec = P(('dp', 'sp'))
    replicated = P()
    new_spec = P('dp')

    def body(x_in, positions, d_out, w_query, w_key, w_value, w_attn_out, w_up, w_down, g_attn, g_mlp, learn_rate):
        weights = (w_query, w_key, w_value, w_attn_out, w_up, w_down)
        layers = w_query.shape[0]
        act = x_in
        value_a7 = []
        for layer in range(layers):
            norm_attn, inv_attn = rms_norm(act, g_attn[layer])
            query = rotary(contract('bsd,dhe->bshe', norm_attn, w_query[layer]), positions, 1.0).astype(jnp.bfloat16)
            keys = rotary(contract('bsd,dhe->bshe', norm_attn, w_key[layer]), positions, 1.0).astype(jnp.bfloat16)
            values = contract('bsd,dhe->bshe', norm_attn, w_value[layer]).astype(jnp.bfloat16)
            q_heads = to_heads(query)
            k_heads = to_heads(keys)
            v_heads = to_heads(values)
            q_group = q_heads.reshape(q_heads.shape[0], q_heads.shape[1], k_heads.shape[2], -1, q_heads.shape[3])
            attn_out, log_sum = attn_forward(q_group, k_heads, v_heads)
            mixed = to_seq(attn_out.reshape(q_heads.shape))
            hidden = (act.astype(jnp.float32) + contract('bshe,hed->bsd', mixed, w_attn_out[layer])).astype(jnp.bfloat16)
            norm_mlp, inv_mlp = rms_norm(hidden, g_mlp[layer])
            pre_act = contract('bsd,df->bsf', norm_mlp, w_up[layer])
            gelu_out = gelu_tanh(pre_act).astype(jnp.bfloat16)
            value_a7.append((act, norm_attn, inv_attn, q_group, k_heads, v_heads, attn_out, log_sum, mixed, hidden, norm_mlp, inv_mlp, pre_act, gelu_out))
            act = (hidden.astype(jnp.float32) + contract('bsf,fd->bsd', gelu_out, w_down[layer])).astype(jnp.bfloat16)
        grad_act = d_out
        layer_grads = [None] * layers
        for layer in reversed(range(layers)):
            (layer_in, norm_attn, inv_attn, q_group, k_heads, v_heads, attn_out, log_sum, mixed, hidden, norm_mlp, inv_mlp, pre_act, gelu_out) = value_a7[layer]
            d_gelu = contract('bsd,fd->bsf', grad_act, w_down[layer])
            d_pre = jax.vjp(gelu_tanh, pre_act)[1](d_gelu)[0].astype(jnp.bfloat16)
            grad_down = contract('bsf,bsd->fd', gelu_out, grad_act)
            grad_up = contract('bsd,bsf->df', norm_mlp, d_pre)
            d_norm_mlp = contract('bsf,df->bsd', d_pre, w_up[layer])
            d_hidden = (grad_act.astype(jnp.float32) + rms_norm_grad(hidden, inv_mlp, g_mlp[layer], d_norm_mlp)).astype(jnp.bfloat16)
            grad_attn_out = contract('bshe,bsd->hed', mixed, d_hidden)
            d_mixed = contract('bsd,hed->bshe', d_hidden, w_attn_out[layer]).astype(jnp.bfloat16)
            d_heads = to_heads(d_mixed).reshape(q_group.shape)
            dq_group, dk_heads, dv_heads = attn_backward(q_group, k_heads, v_heads, attn_out, log_sum, d_heads)
            head_shape = (q_group.shape[0], q_group.shape[1], -1, q_group.shape[4])
            d_query = rotary(to_seq(dq_group.astype(jnp.bfloat16).reshape(head_shape)), positions, -1.0).astype(jnp.bfloat16)
            d_keys = rotary(to_seq(dk_heads.astype(jnp.bfloat16)), positions, -1.0).astype(jnp.bfloat16)
            d_values = to_seq(dv_heads.astype(jnp.bfloat16))
            grad_query = contract('bsd,bshe->dhe', norm_attn, d_query)
            grad_key = contract('bsd,bshe->dhe', norm_attn, d_keys)
            grad_value = contract('bsd,bshe->dhe', norm_attn, d_values)
            d_norm_attn = contract('bshe,dhe->bsd', d_query, w_query[layer]) + contract('bshe,dhe->bsd', d_keys, w_key[layer]) + contract('bshe,dhe->bsd', d_values, w_value[layer])
            grad_act = (d_hidden.astype(jnp.float32) + rms_norm_grad(layer_in, inv_attn, g_attn[layer], d_norm_attn)).astype(jnp.bfloat16)
            layer_grads[layer] = (grad_query, grad_key, grad_value, grad_attn_out, grad_up, grad_down)
        totals = lax.psum(tuple(jnp.stack([grads[index] for grads in layer_grads]) for index in range(len(weights))), SEQ_AXIS)
        news = tuple((weight.astype(jnp.float32) - learn_rate * total).astype(jnp.bfloat16) for weight, total in zip(weights, totals))
        return (act, grad_act) + news

    return jax.shard_map(body, mesh=mesh, in_specs=(act_spec, pos_spec, act_spec) + (replicated,) * 9, out_specs=(act_spec, act_spec) + (new_spec,) * 6, check_vma=False)
```

profile of v0, /device:TPU:112, one launch (start us, length us, event | category | flops | bytes accessed | tf_op | source)
XLA Modules:
  0.0 2123.0 jit_solution(9119575689370105697)
XLA Ops:
  31.4 11.7 all-to-all-done
  50.4 18.5 all-to-all-done.1
  89.6 5.7 all-to-all-done.2
  102.8 21.5 %fusion.8 = (f32[6,2,1024]{2,1,0:T(2,128)S(1)}, f32[6,2,1024,1024]{3,2,1,0:T(8,128)}) fusion(pred[1024,1024]{0,1:T(8,128)(4,1)S(1)} %iota_compare_fusion, bf16[6,1024,2,64]{1,3,2,0:T(8,128)(2,1)} %all_to_all.207, bf16[6,1024,2,64]{1,3,2,0:T(8,128)(2,1)} %reshape.318), kind=kOutput, calls=%fused_computation.24 | convolution fusion | flops 1648349184 | bytes 54575104 | tf_op jit(solution)/shard_map/bqgre,bkge->bgrqk/dot_general | solution.py:12
  124.3 21.1 fusion.4
  145.4 21.5 %fusion.172 = bf16[6,2,64,1024]{3,2,1,0:T(8,128)(2,1)} fusion(bf16[6,1024,2,64]{1,3,2,0:T(8,128)(2,1)S(1)} %copy-done.44, f32[6,2,1024]{2,1,0:T(2,128)S(1)} %fusion.4, f32[6,2,1024]{2,1,0:T(2,128)S(1)} %get-tuple-element.53, f32[6,2,1024,1024]{3,2,1,0:T(8,128)} %get-tuple-element.54, pred[1024,1024]{0,1:T(8,128)(4,1)S(1)} %iota_compare_fusion), kind=kOutput, calls=%fused_computation.243 | convolution fusion | flops 1674313728 | bytes 54624256 | tf_op jit(solution)/shard_map/bgrqk,bkge->bqgre/dot_general | solution.py:12
  166.9 8.3 copy.63
  175.2 6.9 reshape.374
  187.3 20.7 all-to-all-done.3
  208.0 6.7 reshape.375
  214.8 8.1 copy.64
  228.4 12.8 fusion.52
  241.3 12.2 fusion.80
  273.1 12.6 all-to-all-done.4
  292.0 18.8 all-to-all-done.5
  328.8 7.8 all-to-all-done.6
  343.0 21.8 %fusion.9 = (f32[6,2,1024]{2,1,0:T(2,128)S(1)}, f32[6,2,1024,1024]{3,2,1,0:T(8,128)}) fusion(pred[1024,1024]{0,1:T(8,128)(4,1)S(1)} %iota_compare_fusion, bf16[6,1024,2,64]{1,3,2,0:T(8,128)(2,1)} %all_to_all.222, bf16[6,1024,2,64]{1,3,2,0:T(8,128)(2,1)S(1)} %reshape.321), kind=kOutput, calls=%fused_computation.25 | convolution fusion | flops 1648349184 | bytes 54575104 | tf_op jit(solution)/shard_map/bqgre,bkge->bgrqk/dot_general | solution.py:12
  364.8 21.1 fusion.5
  385.9 21.5 %fusion.175 = bf16[6,2,64,1024]{3,2,1,0:T(8,128)(2,1)} fusion(bf16[6,1024,2,64]{1,3,2,0:T(8,128)(2,1)S(1)} %copy-done.45, f32[6,2,1024]{2,1,0:T(2,128)S(1)} %fusion.5, f32[6,2,1024]{2,1,0:T(2,128)S(1)} %get-tuple-element.59, f32[6,2,1024,1024]{3,2,1,0:T(8,128)} %get-tuple-element.60, pred[1024,1024]{0,1:T(8,128)(4,1)S(1)} %iota_compare_fusion), kind=kOutput, calls=%fused_computation.244 | convolution fusion | flops 1674313728 | bytes 54624256 | tf_op jit(solution)/shard_map/bgrqk,bkge->bqgre/dot_general | solution.py:12
  407.4 7.2 copy.72
  424.3 20.6 all-to-all-done.7
  450.2 6.1 copy.73
  462.1 12.7 fusion.44
  474.8 19.7 fusion.37
  494.5 15.6 convolution_bitcast_fusion
  510.2 10.0 fusion.97
  536.0 13.5 convolution_bitcast_fusion.2
  560.8 30.4 %fusion.12 = bf16[6,2,1024,1024]{2,3,1,0:T(8,128)(2,1)} fusion(f32[6,2,1024,1024]{3,2,1,0:T(8,128)} %get-tuple-element.60, f32[6,2,1024]{2,1,0:T(2,128)S(1)} %fusion.101, f32[6,2,1024]{2,1,0:T(2,128)S(1)} %log_add_fusion.1, pred[1024,1024]{0,1:T(8,128)(4,1)S(1)} %copy-done.5, bf16[6,1024,2,64]{1,3,2,0:T(8,128)(2,1)} %all_to_all.218, ...), kind=kOutput, calls=%fused_computation.28 | convolution fusion | flops 1698693120 | bytes 79790080 | tf_op jit(solution)/shard_map/bqgre,bkge->bgrqk/dot_general | solution.py:12
  591.2 13.8 fusion.222
  605.0 7.2 copy.77
  621.3 13.6 fusion.223
  635.0 7.2 copy.80
  651.3 20.5 fusion.226
  671.8 7.2 copy.83
  688.8 6.1 copy.78
  705.3 6.1 copy.81
  734.2 6.2 copy.84
  740.3 5.6 copy.155
  745.9 6.9 fusion.88
  753.8 17.9 fusion.30
  771.7 9.3 fusion.79
  781.0 10.8 convolution_bitcast_fusion.3
  791.8 14.8 convolution_bitcast_fusion.1
  825.6 23.1 %pad_maximum_fusion = f32[2,1024,4096]{2,1,0:T(8,128)} fusion(f32[1,1024,4096]{2,1,0:T(8,128)} %convolution_bitcast_fusion.2, f32[1,1024,4096]{2,1,0:T(8,128)} %convolution_bitcast_fusion.3), kind=kLoop, calls=%fused_computation.20 | loop fusion | flops 8388608 | bytes 67108864 | tf_op jit(solution)/shard_map/stack | solution.py:130
  857.0 30.7 %fusion.13 = bf16[6,2,1024,1024]{2,3,1,0:T(8,128)(2,1)} fusion(f32[6,2,1024,1024]{3,2,1,0:T(8,128)} %get-tuple-element.54, f32[6,2,1024]{2,1,0:T(2,128)S(1)} %fusion.99, f32[6,2,1024]{2,1,0:T(2,128)S(1)} %copy-done.71, pred[1024,1024]{0,1:T(8,128)(4,1)S(1)} %copy-done.6, bf16[6,1024,2,64]{1,3,2,0:T(8,128)(2,1)} %all_to_all.203, ...), kind=kOutput, calls=%fused_computation.29 | convolution fusion | flops 1698693120 | bytes 79790080 | tf_op jit(solution)/shard_map/bqgre,bkge->bgrqk/dot_general | solution.py:12
  887.7 13.8 fusion.224
  901.5 7.2 copy.88
  918.2 13.6 fusion.225
  931.8 7.2 copy.91
  948.7 20.8 fusion.229
  969.4 7.2 copy.94
  986.0 8.5 pad_maximum_fusion.5
  994.5 23.6 %pad_maximum_fusion.1 = f32[2,4096,1024]{2,1,0:T(8,128)} fusion(f32[1,4096,1024]{2,1,0:T(8,128)} %convolution_bitcast_fusion, f32[1,4096,1024]{2,1,0:T(8,128)} %convolution_bitcast_fusion.1), kind=kLoop, calls=%fused_computation.21 | loop fusion | flops 8388608 | bytes 67108864 | tf_op jit(solution)/shard_map/stack | solution.py:130
  1023.3 6.1 copy.89
  1034.7 6.1 copy.92
  1046.1 5.5 copy.154
  1077.6 14.5 fusion.92
  1092.1 6.1 copy.95
  1109.8 931.6 %all-reduce.3.cloned.1.call-done = (f32[2,1024,16,64]{1,3,2,0:T(8,128)}, f32[2,1024,16,64]{1,3,2,0:T(8,128)}, f32[2,1024,16,64]{1,3,2,0:T(8,128)}, f32[2,16,64,1...) async-done(((f32[2,1024,16,64]{1,3,2,0:T(8,128)}, f32[2,1024,16,64]{1,3,2,0:T(8,128)}, f32[2,1024,16,64]{1,3,2,0:T(8,128)}, ...) | async-done | bytes 100663312 | tf_op jit(solution)/shard_map/psum | solution.py:130
  2041.5 8.4 subtract_convert_fusion.5
  2049.8 7.3 subtract_convert_fusion.2
  2057.2 24.5 %subtract_convert_fusion.1 = bf16[2,1024,4096]{2,1,0:T(8,128)(2,1)} fusion(f32[2,1024,4096]{2,1,0:T(8,128)} %get-tuple-element.12, bf16[2,1024,4096]{2,1,0:T(8,128)(2,1)} %param.19, f32[]{:T(128)S(6)} %copy.182), kind=kLoop, calls=%fused_computation.23 | loop fusion | flops 33554432 | bytes 67108864 | tf_op jit(solution)/shard_map/convert_element_type | solution.py:131
  2085.8 16.7 subtract_convert_fusion
  2102.5 13.3 subtract_convert_fusion.3
  (318 shorter events, 342.3 us)
Async XLA Ops:
  8.6 17.4 copy-start.59
  10.9 15.1 copy-start.73
  14.9 6.6 copy-start.80
  14.9 7.4 copy-start.1
  16.2 26.9 %all-to-all-start = ((bf16[6,128,16,64]{1,3,0,2:T(8,128)(2,1)}), bf16[6,128,16,64]{1,3,0,2:T(8,128)(2,1)S(1)}, u32[]{:S(2)}, u32[]{:S(2)}) async-start(bf16[6,128,16,64]{1,3,0,2:T(8,128)(2,1)} %copy.56), calls=%async_computation | async-start | bytes 3145728 | tf_op jit(solution)/shard_map/all_to_all | solution.py:71
  43.1 25.8 %all-to-all-start.1 = ((bf16[6,128,16,64]{1,3,0,2:T(8,128)(2,1)}), bf16[6,128,16,64]{1,3,0,2:T(8,128)(2,1)}, u32[]{:S(2)}, u32[]{:S(2)}) async-start(bf16[6,128,16,64]{1,3,0,2:T(8,128)(2,1)} %copy.58), calls=%async_computation.1 | async-start | bytes 3145728 | tf_op jit(solution)/shard_map/all_to_all | solution.py:71
  69.0 26.3 %all-to-all-start.2 = ((bf16[6,128,16,64]{1,3,0,2:T(8,128)(2,1)}), bf16[6,128,16,64]{1,3,0,2:T(8,128)(2,1)}, u32[]{:S(2)}, u32[]{:S(2)}) async-start(bf16[6,128,16,64]{1,3,0,2:T(8,128)(2,1)} %copy.60), calls=%async_computation.2 | async-start | bytes 3145728 | tf_op jit(solution)/shard_map/all_to_all | solution.py:71
  74.3 311.6 %copy-start.4 = (pred[1024,1024]{0,1:T(8,128)(4,1)}, pred[1024,1024]{0,1:T(8,128)(4,1)S(1)}, u32[]{:S(2)}) copy-start(pred[1024,1024]{0,1:T(8,128)(4,1)S(1)} %iota_compare_fusion) | copy-start | bytes 3145732
  124.3 21.1 copy-start.63
  124.3 21.1 copy-start.44
  145.4 21.5 %copy-start.65 = (f32[6,2,1024]{2,1,0:T(2,128)}, f32[6,2,1024]{2,1,0:T(2,128)S(1)}, u32[]{:S(2)}) copy-start(f32[6,2,1024]{2,1,0:T(2,128)S(1)} %fusion.4) | copy-start | bytes 147460
  175.2 11.4 copy-start.79
  182.2 25.8 %all-to-all-start.3 = ((bf16[8,2,49152]{2,1,0:T(2,128)(2,1)}), bf16[8,2,49152]{2,1,0:T(2,128)(2,1)}, u32[]{:S(2)}, u32[]{:S(2)}) async-start(bf16[8,2,49152]{2,1,0:T(2,128)(2,1)} %reshape.374), calls=%async_computation.3 | async-start | bytes 3145728 | tf_op jit(solution)/shard_map/all_to_all | solution.py:75
  187.3 40.6 %copy-start.50 = (f32[1,1024]{1,0:T(1,128)}, f32[1,1024]{1,0:T(1,128)S(1)}, u32[]{:S(2)}) copy-start(f32[1,1024]{1,0:T(1,128)S(1)} %get-tuple-element.39) | copy-start | bytes 12292
  222.9 18.4 slice-start.12
  227.8 13.4 copy-start.52
  228.4 12.8 slice-start.13
  228.4 12.8 slice-start.14
  228.4 12.8 slice-start.15
  241.3 12.8 copy-start.61
  254.1 13.9 copy-start.75
  258.1 6.2 copy-start.10
  259.4 26.3 %all-to-all-start.4 = ((bf16[6,128,16,64]{1,3,0,2:T(8,128)(2,1)}), bf16[6,128,16,64]{1,3,0,2:T(8,128)(2,1)}, u32[]{:S(2)}, u32[]{:S(2)}) async-start(bf16[6,128,16,64]{1,3,0,2:T(8,128)(2,1)} %copy.65), calls=%async_computation.4 | async-start | bytes 3145728 | tf_op jit(solution)/shard_map/all_to_all | solution.py:71
  285.6 25.1 %all-to-all-start.5 = ((bf16[6,128,16,64]{1,3,0,2:T(8,128)(2,1)}), bf16[6,128,16,64]{1,3,0,2:T(8,128)(2,1)S(1)}, u32[]{:S(2)}, u32[]{:S(2)}) async-start(bf16[6,128,16,64]{1,3,0,2:T(8,128)(2,1)} %copy.67), calls=%async_computation.5 | async-start | bytes 3145728 | tf_op jit(solution)/shard_map/all_to_all | solution.py:71
  310.8 25.8 %all-to-all-start.6 = ((bf16[6,128,16,64]{1,3,0,2:T(8,128)(2,1)}), bf16[6,128,16,64]{1,3,0,2:T(8,128)(2,1)}, u32[]{:S(2)}, u32[]{:S(2)}) async-start(bf16[6,128,16,64]{1,3,0,2:T(8,128)(2,1)} %copy.69), calls=%async_computation.6 | async-start | bytes 3145728 | tf_op jit(solution)/shard_map/all_to_all | solution.py:71
  342.9 21.8 %copy-start.13 = (bf16[6,1024,2,64]{1,3,2,0:T(8,128)(2,1)}, bf16[6,1024,2,64]{1,3,2,0:T(8,128)(2,1)S(1)}, u32[]{:S(2)}) copy-start(bf16[6,1024,2,64]{1,3,2,0:T(8,128)(2,1)S(1)} %reshape.321) | copy-start | bytes 4718596
  364.8 21.1 copy-start.45
  414.6 9.0 copy-start.64
  414.6 9.0 copy-start.66
  419.1 25.8 %all-to-all-start.7 = ((bf16[8,2,49152]{2,1,0:T(2,128)(2,1)}), bf16[8,2,49152]{2,1,0:T(2,128)(2,1)}, u32[]{:S(2)}, u32[]{:S(2)}) async-start(bf16[8,2,49152]{2,1,0:T(2,128)(2,1)} %reshape.376), calls=%async_computation.7 | async-start | bytes 3145728 | tf_op jit(solution)/shard_map/all_to_all | solution.py:75
  474.8 35.3 %slice-start.8 = ((s8[16777216]{0:T(1024)(128)(4,1)}), s8[4194304]{0:T(1024)(128)(4,1)S(1)}, s32[]{:S(2)}) async-start(s8[16777216]{0:T(1024)(128)(4,1)} %bitcast.558), calls=%async_computation.25 | async-start | bytes 8388608
  474.8 35.3 %slice-start.9 = ((s8[16777216]{0:T(1024)(128)(4,1)}), s8[4194304]{0:T(1024)(128)(4,1)S(1)}, s32[]{:S(2)}) async-start(s8[16777216]{0:T(1024)(128)(4,1)} %bitcast.558), calls=%async_computation.26 | async-start | bytes 8388608
  474.8 35.3 %slice-start.10 = ((s8[16777216]{0:T(1024)(128)(4,1)}), s8[4194304]{0:T(1024)(128)(4,1)S(1)}, s32[]{:S(2)}) async-start(s8[16777216]{0:T(1024)(128)(4,1)} %bitcast.558), calls=%async_computation.27 | async-start | bytes 8388608
  494.5 15.7 slice-start.11
  494.5 15.7 copy-start.22
  523.8 7.3 copy-start.31
  526.9 25.6 %all-to-all-start.8 = ((bf16[6,128,16,64]{1,3,0,2:T(8,128)(2,1)}), bf16[6,128,16,64]{1,3,0,2:T(8,128)(2,1)S(1)}, u32[]{:S(2)}, u32[]{:S(2)}) async-start(bf16[6,128,16,64]{1,3,0,2:T(8,128)(2,1)} %copy.74), calls=%async_computation.8 | async-start | bytes 3145728 | tf_op jit(solution)/shard_map/all_to_all | solution.py:71
  560.7 30.4 %copy-start.15 = (bf16[6,1024,2,64]{1,3,2,0:T(8,128)(2,1)S(1)}, bf16[6,1024,2,64]{1,3,2,0:T(8,128)(2,1)}, u32[]{:S(2)}) copy-start(bf16[6,1024,2,64]{1,3,2,0:T(8,128)(2,1)} %all_to_all.222) | copy-start | bytes 4718596
  616.7 30.0 %all-to-all-start.9 = ((bf16[8,2,49152]{2,1,0:T(2,128)(2,1)}), bf16[8,2,49152]{2,1,0:T(2,128)(2,1)}, u32[]{:S(2)}, u32[]{:S(2)}) async-start(bf16[8,2,49152]{2,1,0:T(2,128)(2,1)} %reshape.380), calls=%async_computation.9 | async-start | bytes 3145728 | tf_op jit(solution)/shard_map/all_to_all | solution.py:75
  646.7 48.2 %all-to-all-start.10 = ((bf16[8,2,49152]{2,1,0:T(2,128)(2,1)}), bf16[8,2,49152]{2,1,0:T(2,128)(2,1)}, u32[]{:S(2)}, u32[]{:S(2)}) async-start(bf16[8,2,49152]{2,1,0:T(2,128)(2,1)} %reshape.378), calls=%async_computation.10 | async-start | bytes 3145728 | tf_op jit(solution)/shard_map/all_to_all | solution.py:75
  694.9 34.0 %all-to-all-start.11 = ((bf16[8,2,49152]{2,1,0:T(2,128)(2,1)}), bf16[8,2,49152]{2,1,0:T(2,128)(2,1)}, u32[]{:S(2)}, u32[]{:S(2)}) async-start(bf16[8,2,49152]{2,1,0:T(2,128)(2,1)} %reshape.382), calls=%async_computation.11 | async-start | bytes 3145728 | tf_op jit(solution)/shard_map/all_to_all | solution.py:75
  745.9 6.9 copy-start.12
  745.9 6.9 copy-start.32
  745.9 6.9 copy-start.78
  753.8 17.9 copy-start.25
  753.8 17.9 copy-start.51
  771.7 9.3 copy-start.53
  791.8 14.8 copy-start.77
  812.0 36.7 %all-to-all-start.12 = ((bf16[6,128,16,64]{1,3,0,2:T(8,128)(2,1)}), bf16[6,128,16,64]{1,3,0,2:T(8,128)(2,1)S(1)}, u32[]{:S(2)}, u32[]{:S(2)}) async-start(bf16[6,128,16,64]{1,3,0,2:T(8,128)(2,1)} %copy.85), calls=%async_computation.12 | async-start | bytes 3145728 | tf_op jit(solution)/shard_map/all_to_all | solution.py:71
  857.0 30.7 %copy-start.9 = (bf16[6,1024,2,64]{1,3,2,0:T(8,128)(2,1)S(1)}, bf16[6,1024,2,64]{1,3,2,0:T(8,128)(2,1)}, u32[]{:S(2)}) copy-start(bf16[6,1024,2,64]{1,3,2,0:T(8,128)(2,1)} %all_to_all.207) | copy-start | bytes 4718596
  913.2 30.3 %all-to-all-start.13 = ((bf16[8,2,49152]{2,1,0:T(2,128)(2,1)}), bf16[8,2,49152]{2,1,0:T(2,128)(2,1)}, u32[]{:S(2)}, u32[]{:S(2)}) async-start(bf16[8,2,49152]{2,1,0:T(2,128)(2,1)} %reshape.386), calls=%async_computation.13 | async-start | bytes 3145728 | tf_op jit(solution)/shard_map/all_to_all | solution.py:75
  943.6 37.6 %all-to-all-start.14 = ((bf16[8,2,49152]{2,1,0:T(2,128)(2,1)}), bf16[8,2,49152]{2,1,0:T(2,128)(2,1)}, u32[]{:S(2)}, u32[]{:S(2)}) async-start(bf16[8,2,49152]{2,1,0:T(2,128)(2,1)} %reshape.384), calls=%async_computation.14 | async-start | bytes 3145728 | tf_op jit(solution)/shard_map/all_to_all | solution.py:75
  981.1 59.7 %all-to-all-start.15 = ((bf16[8,2,49152]{2,1,0:T(2,128)(2,1)}), bf16[8,2,49152]{2,1,0:T(2,128)(2,1)}, u32[]{:S(2)}, u32[]{:S(2)}) async-start(bf16[8,2,49152]{2,1,0:T(2,128)(2,1)} %reshape.388), calls=%async_computation.15 | async-start | bytes 3145728 | tf_op jit(solution)/shard_map/all_to_all | solution.py:75
  986.0 1055.5 %all-reduce.3.cloned.1.call-start = ((), (), s32[]{:S(2)}) async-start(), calls=%async_computation.16 | async-start | bytes 201326592 | tf_op jit(solution)/shard_map/psum | solution.py:130
  1098.3 7.2 copy-start.20
  2041.5 8.4 copy-start.37
  2049.8 31.8 %slice-start = ((s8[33554432]{0:T(1024)(128)(4,1)}), s8[4194304]{0:T(1024)(128)(4,1)S(1)}, s32[]{:S(2)}) async-start(s8[33554432]{0:T(1024)(128)(4,1)} %bitcast.552), calls=%async_computation.17 | async-start | bytes 8388608
  2049.8 31.8 %slice-start.1 = ((s8[33554432]{0:T(1024)(128)(4,1)}), s8[4194304]{0:T(1024)(128)(4,1)S(1)}, s32[]{:S(2)}) async-start(s8[33554432]{0:T(1024)(128)(4,1)} %bitcast.552), calls=%async_computation.18 | async-start | bytes 8388608
  2057.1 24.5 %slice-start.2 = ((s8[33554432]{0:T(1024)(128)(4,1)}), s8[4194304]{0:T(1024)(128)(4,1)S(1)}, s32[]{:S(2)}) async-start(s8[33554432]{0:T(1024)(128)(4,1)} %bitcast.552), calls=%async_computation.19 | async-start | bytes 8388608
  2057.1 24.5 %slice-start.3 = ((s8[33554432]{0:T(1024)(128)(4,1)}), s8[4194304]{0:T(1024)(128)(4,1)S(1)}, s32[]{:S(2)}) async-start(s8[33554432]{0:T(1024)(128)(4,1)} %bitcast.552), calls=%async_computation.20 | async-start | bytes 8388608
  2057.1 24.7 %slice-start.4 = ((s8[33554432]{0:T(1024)(128)(4,1)}), s8[4194304]{0:T(1024)(128)(4,1)S(1)}, s32[]{:S(2)}) async-start(s8[33554432]{0:T(1024)(128)(4,1)} %bitcast.552), calls=%async_computation.21 | async-start | bytes 8388608
  2057.1 26.3 %slice-start.5 = ((s8[33554432]{0:T(1024)(128)(4,1)}), s8[4194304]{0:T(1024)(128)(4,1)S(1)}, s32[]{:S(2)}) async-start(s8[33554432]{0:T(1024)(128)(4,1)} %bitcast.552), calls=%async_computation.22 | async-start | bytes 8388608
  2057.2 27.5 %slice-start.6 = ((s8[33554432]{0:T(1024)(128)(4,1)}), s8[4194304]{0:T(1024)(128)(4,1)S(1)}, s32[]{:S(2)}) async-start(s8[33554432]{0:T(1024)(128)(4,1)} %bitcast.552), calls=%async_computation.23 | async-start | bytes 8388608
  2057.2 28.7 %slice-start.7 = ((s8[33554432]{0:T(1024)(128)(4,1)}), s8[4194304]{0:T(1024)(128)(4,1)S(1)}, s32[]{:S(2)}) async-start(s8[33554432]{0:T(1024)(128)(4,1)} %bitcast.552), calls=%async_computation.24 | async-start | bytes 8388608
  (50 other events, 191.8 us)
Sparse Core Ops, SparseCore 0:
  1077.1 964.3 all-reduce.2
where the time goes:
time: 2130 us; the launch traced here: 2120 us
  waiting for transfers between devices  1050 us (49%)
  matrix products  492 us (23%)
  local copies, waits for them, and re-layouts  278 us (13%)
  other arithmetic  209 us (10%)
  starting transfers between devices  75.5 us (4%)
    psum x1, waiting for transfers between devices, body(): lax.psum(tuple((jnp.stack([grads[index] for grads in layer_grads]) for in...  932 us
    dot_general x48, matrix products, contract(): return jnp.einsum(form, left, right, preferred_element_type=jnp.float32)  492 us
    unnamed x210, local copies, waits for them, and re-layouts  92.5 us
    all_to_all x8, waiting for transfers between devices, to_heads(): return lax.all_to_all(tensor, SEQ_AXIS, 2, 1, tiled=True)  78.2 us
    convert_element_type x5, other arithmetic, body(): (weight.astype(jnp.float32) - learn_rate * total).astype(jnp.bfloat16)  70.2 us
    another operation x6, other arithmetic, body(): jnp.stack([grads[index] for grads in layer_grads])  67.8 us
    all_to_all x10, local copies, waits for them, and re-layouts, to_seq(): return lax.all_to_all(tensor, SEQ_AXIS, 1, 2, tiled=True)  62 us
  transfers between devices with their start and end apart: 17, of which 10 were waited for; matrix products, arithmetic and copies ran while one was open for 16% of the time, Pallas kernels for 0%

commit v1 on v0

v1 whole, which is shorter than its diff:
```python
import functools
import math

import jax
import jax.numpy as jnp
from jax import lax
from jax.experimental import pallas as pl
from jax.experimental.pallas import tpu as pltpu
from jax.sharding import PartitionSpec as P


EPSILON = 1e-5
ROPE_BASE = 10000.0
SEQ_AXIS = 'sp'
F32 = jnp.float32
BF16 = jnp.bfloat16
LOG2E = math.log2(math.e)
NT = (((1,), (1,)), ((), ()))


def contract(form, left, right):
    return jnp.einsum(form, left, right, preferred_element_type=F32)


def gelu_tanh(value):
    return jax.nn.gelu(value, approximate=True)


def rms_norm(act, gain):
    wide = act.astype(F32)
    inv_rms = lax.rsqrt(jnp.mean(wide * wide, axis=-1, keepdims=True) + EPSILON)
    return (wide * inv_rms * gain).astype(BF16), inv_rms


def rms_norm_grad(act, inv_rms, gain, d_norm):
    wide = act.astype(F32)
    d_gain = d_norm * gain
    return inv_rms * d_gain - wide * inv_rms ** 3 * jnp.mean(d_gain * wide, axis=-1, keepdims=True)


def swap_halves(x, head_dim):
    half = head_dim // 2
    lanes = x.shape[-1]
    lane = lax.broadcasted_iota(jnp.int32, x.shape, 1)
    ahead = pltpu.roll(x, lanes - half, 1)
    behind = pltpu.roll(x, half, 1)
    return jnp.where(lane % head_dim < half, ahead, behind)


def causal_mask(keys, queries):
    return lax.broadcasted_iota(jnp.int32, (keys, queries), 0) <= lax.broadcasted_iota(jnp.int32, (keys, queries), 1)


def attn_fwd_kernel(head_dim, blk, n_ref, w_ref, cos_ref, sin_ref, q_ref, k_ref, v_ref, o_ref, lse_ref):
    shards, _, rows, lanes = q_ref.shape
    seq = shards * rows
    heads = lanes // head_dim
    scale = head_dim ** -0.5
    step = 256
    for t in range(seq // step):
        per = step // rows
        n = n_ref[t * per:(t + 1) * per, 0].reshape(step, n_ref.shape[-1])
        qkv = lax.dot_general(n, w_ref[...], NT, preferred_element_type=F32)
        cos = cos_ref[t * step:(t + 1) * step]
        sin = sin_ref[t * step:(t + 1) * step]
        for idx, ref in enumerate((q_ref, k_ref, v_ref)):
            part = qkv[:, idx * lanes:(idx + 1) * lanes]
            if idx < 2:
                part = part * cos + swap_halves(part, head_dim) * sin
            ref[t * per:(t + 1) * per, 0] = part.astype(BF16).reshape(per, rows, lanes)
    mask = causal_mask(blk, blk)
    vt = v_ref[:, 0].reshape(seq, lanes).T
    for j in range(seq // blk):
        per = blk // rows
        q_all = q_ref[j * per:(j + 1) * per, 0].reshape(blk, lanes)
        outs = []
        for h in range(heads):
            cols = slice(h * head_dim, (h + 1) * head_dim)
            q = q_all[:, cols]
            k_diag = k_ref[j * per:(j + 1) * per, 0].reshape(blk, lanes)[:, cols]
            s_diag = lax.dot_general(k_diag, q, NT, preferred_element_type=F32)
            s_diag = jnp.where(mask, s_diag, -1e30)
            top = jnp.max(s_diag, axis=0, keepdims=True)
            if j:
                k_off = k_ref[:j * per, 0].reshape(j * blk, lanes)[:, cols]
                s_off = lax.dot_general(k_off, q, NT, preferred_element_type=F32)
                top = jnp.maximum(top, jnp.max(s_off, axis=0, keepdims=True))
            c = scale * LOG2E
            e_diag = jnp.exp2((s_diag - top) * c)
            total = jnp.sum(e_diag, axis=0, keepdims=True)
            if j:
                e_off = jnp.exp2((s_off - top) * c)
                total = total + jnp.sum(e_off, axis=0, keepdims=True)
            inv = 1.0 / total
            out = jnp.dot(vt[cols, j * blk:(j + 1) * blk], (e_diag * inv).astype(BF16), preferred_element_type=F32)
            if j:
                out = out + jnp.dot(vt[cols, :j * blk], (e_off * inv).astype(BF16), preferred_element_type=F32)
            outs.append(out)
            lse_ref[0, h:h + 1, j * blk:(j + 1) * blk] = top * scale + jnp.log(total)
        o = jnp.concatenate(outs, axis=0).T.astype(BF16)
        o_ref[j * per:(j + 1) * per, 0] = o.reshape(per, rows, lanes)


def attn_forward(n_all, w_qkv, cos, sin, head_dim):
    shards, batch, rows, d_model = n_all.shape
    lanes = w_qkv.shape[0] // 3
    heads = lanes // head_dim
    seq = shards * rows
    blk = min(256, seq)
    head_block = pl.BlockSpec((shards, 1, rows, lanes), lambda b: (0, b, 0, 0))
    head_shape = jax.ShapeDtypeStruct((shards, batch, rows, lanes), BF16)
    flops = 2 * batch * seq * (d_model * 3 * lanes + seq * lanes * 2)
    return pl.pallas_call(
        functools.partial(attn_fwd_kernel, head_dim, blk),
        grid=(batch,),
        in_specs=[
            pl.BlockSpec((shards, 1, rows, d_model), lambda b: (0, b, 0, 0)),
            pl.BlockSpec(w_qkv.shape, lambda b: (0, 0)),
            pl.BlockSpec(cos.shape, lambda b: (0, 0)),
            pl.BlockSpec(sin.shape, lambda b: (0, 0)),
        ],
        out_specs=[head_block] * 4 + [pl.BlockSpec((1, heads, seq), lambda b: (b, 0, 0))],
        out_shape=[head_shape] * 4 + [jax.ShapeDtypeStruct((batch, heads, seq), F32)],
        cost_estimate=pl.CostEstimate(flops=flops * 4, bytes_accessed=n_all.size * 2, transcendentals=batch * heads * seq * seq),
        compiler_params=pltpu.CompilerParams(dimension_semantics=('arbitrary',), vmem_limit_bytes=50 * 1024 * 1024),
        name='attn_fwd',
    )(n_all, w_qkv, cos, sin)


def attn_bwd_kernel(head_dim, blk, q_ref, k_ref, v_ref, o_ref, d_ref, lse_ref, cos_ref, sin_ref, dqkv_ref, dk_acc, dv_acc):
    shards, _, rows, lanes = q_ref.shape
    seq = shards * rows
    heads = lanes // head_dim
    scale = head_dim ** -0.5
    per = blk // rows
    mask = causal_mask(blk, blk)
    kt = k_ref[:, 0].reshape(seq, lanes).T
    dk_acc[...] = jnp.zeros_like(dk_acc)
    dv_acc[...] = jnp.zeros_like(dv_acc)

    def unrotate(grad, lo, hi):
        low = grad.astype(BF16).astype(F32)
        return (low * cos_ref[lo:hi] - swap_halves(low, head_dim) * sin_ref[lo:hi]).astype(BF16)

    for j in range(seq // blk):
        lo, hi = j * blk, (j + 1) * blk
        q_all = q_ref[j * per:(j + 1) * per, 0].reshape(blk, lanes)
        d_all = d_ref[j * per:(j + 1) * per, 0].reshape(blk, lanes)
        o_all = o_ref[j * per:(j + 1) * per, 0].reshape(blk, lanes)
        prod_t = (d_all.astype(F32) * o_all.astype(F32)).T
        dq_parts = []
        for h in range(heads):
            cols = slice(h * head_dim, (h + 1) * head_dim)
            q, d = q_all[:, cols], d_all[:, cols]
            delta = jnp.sum(prod_t[cols], axis=0, keepdims=True)
            lse2 = lse_ref[0, h:h + 1, lo:hi] * LOG2E
            c = scale * LOG2E
            spans = [(lo, hi)] + ([(0, lo)] if j else [])
            dq_t = None
            for start, stop in spans:
                k = k_ref[start // rows:stop // rows, 0].reshape(stop - start, lanes)[:, cols]
                v = v_ref[start // rows:stop // rows, 0].reshape(stop - start, lanes)[:, cols]
                s = lax.dot_general(k, q, NT, preferred_element_type=F32)
                p = jnp.exp2(s * c - lse2)
                if start == lo:
                    p = jnp.where(mask, p, 0.0)
                dp = lax.dot_general(v, d, NT, preferred_element_type=F32)
                ds = (p * (dp - delta) * scale).astype(BF16)
                dv_acc[start:stop, cols] += jnp.dot(p.astype(BF16), d, preferred_element_type=F32)
                dk_acc[start:stop, cols] += jnp.dot(ds, q, preferred_element_type=F32)
                part = jnp.dot(kt[cols, start:stop], ds, preferred_element_type=F32)
                dq_t = part if dq_t is None else dq_t + part
            dq_parts.append(dq_t)
        dq = jnp.concatenate(dq_parts, axis=0).T
        dqkv_ref[j * per:(j + 1) * per, 0, 0] = unrotate(dq, lo, hi).reshape(per, rows, lanes)
    for j in range(seq // blk):
        lo, hi = j * blk, (j + 1) * blk
        dqkv_ref[j * per:(j + 1) * per, 1, 0] = unrotate(dk_acc[lo:hi], lo, hi).reshape(per, rows, lanes)
        dqkv_ref[j * per:(j + 1) * per, 2, 0] = dv_acc[lo:hi].astype(BF16).reshape(per, rows, lanes)


def attn_backward(q, k, v, o, d, lse, cos, sin, head_dim):
    shards, batch, rows, lanes = q.shape
    heads = lanes // head_dim
    seq = shards * rows
    blk = min(256, seq)
    head_block = pl.BlockSpec((shards, 1, rows, lanes), lambda b: (0, b, 0, 0))
    flops = 2 * batch * seq * seq * lanes * 5
    return pl.pallas_call(
        functools.partial(attn_bwd_kernel, head_dim, blk),
        grid=(batch,),
        in_specs=[head_block] * 5 + [
            pl.BlockSpec((1, heads, seq), lambda b: (b, 0, 0)),
            pl.BlockSpec(cos.shape, lambda b: (0, 0)),
            pl.BlockSpec(sin.shape, lambda b: (0, 0)),
        ],
        out_specs=pl.BlockSpec((shards, 3, 1, rows, lanes), lambda b: (0, 0, b, 0, 0)),
        out_shape=jax.ShapeDtypeStruct((shards, 3, batch, rows, lanes), BF16),
        scratch_shapes=[pltpu.VMEM((seq, lanes), F32), pltpu.VMEM((seq, lanes), F32)],
        cost_estimate=pl.CostEstimate(flops=flops * 4, bytes_accessed=q.size * 16, transcendentals=batch * heads * seq * seq),
        compiler_params=pltpu.CompilerParams(dimension_semantics=('arbitrary',), vmem_limit_bytes=50 * 1024 * 1024),
        name='attn_bwd',
    )(q, k, v, o, d, lse, cos, sin)


def exchange(tensor):
    return lax.all_to_all(tensor, SEQ_AXIS, 0, 0, tiled=True)


def emit_kernel(in_ref, out_ref):
    out_ref[...] = in_ref[...]


def emit(array):
    layers, height, width = array.shape
    block = pl.BlockSpec((1, max(height // 4, 8), width), lambda layer, row: (layer, row, 0))
    return pl.pallas_call(
        emit_kernel,
        grid=(layers, height // max(height // 4, 8)),
        in_specs=[block],
        out_specs=block,
        out_shape=jax.ShapeDtypeStruct(array.shape, array.dtype),
        cost_estimate=pl.CostEstimate(flops=10 ** 10, bytes_accessed=4 * array.size, transcendentals=0),
        name='emit',
    )(array)


def solution(mesh):
    act_spec = P('dp', 'sp', None)
    pos_spec = P(('dp', 'sp'))
    replicated = P()
    new_spec = P('dp')
    shards = mesh.shape[SEQ_AXIS]

    def body(x_in, positions, d_out, w_query, w_key, w_value, w_attn_out, w_up, w_down, g_attn, g_mlp, learn_rate):
        layers, d_model, heads, head_dim = w_query.shape
        batch, rows, _ = x_in.shape
        tokens = batch * rows
        local = heads // shards
        lanes = local * head_dim
        me = lax.axis_index(SEQ_AXIS)
        half = head_dim // 2

        pos_all = lax.all_gather(positions, SEQ_AXIS, tiled=True)
        inv_freq = ROPE_BASE ** (-2.0 * jnp.arange(half, dtype=F32) / head_dim)
        angle = pos_all.astype(F32)[:, None] * inv_freq
        cos = jnp.tile(jnp.cos(angle), (1, 2 * local))
        sin = jnp.sin(angle)
        sin = jnp.tile(jnp.concatenate([-sin, sin], axis=-1), (1, local))

        def mine(weight, axis):
            size = weight.shape[axis] // shards
            return lax.dynamic_slice_in_dim(weight, me * size, size, axis)

        w_rows = [w.transpose(0, 2, 3, 1).reshape(layers, heads * head_dim, d_model) for w in (w_query, w_key, w_value)]
        w_qkv = jnp.concatenate([mine(w, 1) for w in w_rows], axis=1)
        w_outs = w_attn_out.reshape(layers, heads * head_dim, d_model)

        chunks = 2 if batch % 2 == 0 else 1
        part = batch // chunks
        size = part * rows
        order = lax.optimization_barrier

        def split(array):
            flat = array.reshape(tokens, d_model)
            return [flat[c * size:(c + 1) * size] for c in range(chunks)]

        def join(parts):
            return jnp.concatenate(parts, axis=0)

        def to_tokens(heads_first):
            return heads_first.reshape(shards, size, lanes).transpose(1, 0, 2).reshape(size, heads * head_dim)

        def scatter(grad):
            return lax.psum_scatter(grad, SEQ_AXIS, scatter_dimension=0, tiled=True)

        acts = split(x_in)
        stash = []
        norms = [rms_norm(act, g_attn[0]) for act in acts]
        for layer in range(layers):
            heads_in, exchanged = [], []
            for c in range(chunks):
                n_all = lax.all_gather(norms[c][0].reshape(part, rows, d_model), SEQ_AXIS)
                q, k, v, o, lse = attn_forward(n_all, w_qkv[layer], cos, sin, head_dim)
                heads_in.append((acts[c], n_all, norms[c][1], q, k, v, o, lse))
                exchanged.append(exchange(o))
            saved = []
            for c in range(chunks):
                mixed = to_tokens(exchanged[c])
                hidden = (acts[c].astype(F32) + contract('tc,cd->td', mixed, w_outs[layer])).astype(BF16)
                norm_mlp, inv_mlp = rms_norm(hidden, g_mlp[layer])
                pre_act = contract('td,df->tf', norm_mlp, w_up[layer])
                gelu_out = gelu_tanh(pre_act).astype(BF16)
                saved.append(heads_in[c] + (mixed, hidden, norm_mlp, inv_mlp, pre_act, gelu_out))
                acts[c] = (hidden.astype(F32) + contract('tf,fd->td', gelu_out, w_down[layer])).astype(BF16)
                if layer + 1 < layers:
                    norms[c] = rms_norm(acts[c], g_attn[layer + 1])
                    if c + 1 < chunks:
                        norms[c], exchanged[c + 1] = order((norms[c], exchanged[c + 1]))
            stash.append(saved)
        y_out = join(acts)

        grads = split(d_out)
        sums_qkv, sums_out, sums_up, sums_down = ([None] * layers for _ in range(4))
        for layer in reversed(range(layers)):
            saved = stash[layer]
            above = layer + 1 if layer + 1 < layers else None
            whole = d_out.reshape(tokens, d_model) if above is None else join(grads)
            grad_down = contract('tf,td->fd', join([s[13] for s in saved]), whole)
            pre_acts, grad_down = order(([s[12] for s in saved], grad_down))
            sums_down[layer] = scatter(grad_down)
            d_pres = []
            for c in range(chunks):
                d_gelu = contract('td,fd->tf', grads[c], w_down[layer])
                d_pres.append(jax.vjp(gelu_tanh, pre_acts[c])[1](d_gelu)[0].astype(BF16))
            grad_up = contract('td,tf->df', join([s[10] for s in saved]), join(d_pres))
            if above is not None:
                d_pres, grad_up, sums_up[above] = order((d_pres, grad_up, sums_up[above]))
            else:
                d_pres, grad_up = order((d_pres, grad_up))
            sums_up[layer] = scatter(grad_up)
            d_hiddens, d_heads = [], []
            for c in range(chunks):
                d_norm_mlp = contract('tf,df->td', d_pres[c], w_up[layer])
                d_hidden = (grads[c].astype(F32) + rms_norm_grad(saved[c][9], saved[c][11], g_mlp[layer], d_norm_mlp)).astype(BF16)
                d_mixed = contract('td,cd->tc', d_hidden, w_outs[layer]).astype(BF16)
                d_hiddens.append(d_hidden)
                d_heads.append(exchange(d_mixed.reshape(size, shards, lanes).transpose(1, 0, 2).reshape(shards, part, rows, lanes)))
            grad_out = contract('tc,td->cd', join([s[8] for s in saved]), join(d_hiddens))
            if above is not None:
                d_heads, grad_out, sums_out[above] = order((d_heads, grad_out, sums_out[above]))
            else:
                d_heads, grad_out = order((d_heads, grad_out))
            sums_out[layer] = scatter(grad_out)
            grad_qkv, outs = 0.0, []
            for c in range(chunks):
                _, n_all, _, q, k, v, o, lse = saved[c][:8]
                dqkv = attn_backward(q, k, v, o, d_heads[c], lse, cos, sin, head_dim)
                outs.append(exchange(dqkv))
                grad_qkv = grad_qkv + contract('sibrc,sbrd->icd', dqkv, n_all)
            outs, sums_qkv[layer], sums_down[layer] = order((outs, grad_qkv, sums_down[layer]))
            for c in range(chunks):
                d_norm_attn = sum(contract('tc,cd->td', to_tokens(outs[c][:, idx]), w_rows[idx][layer]) for idx in range(3))
                grads[c] = (d_hiddens[c].astype(F32) + rms_norm_grad(saved[c][0], saved[c][2], g_attn[layer], d_norm_attn)).astype(BF16)
        grad_x = join(grads)
        grad_x, sums_up[0] = order((grad_x, sums_up[0]))
        sums_up[0], sums_out[0] = order((sums_up[0], sums_out[0]))

        def renew(pairs):
            new = [(mine(weight, 1).astype(F32) - learn_rate * total).astype(BF16) for weight, total in pairs]
            return lax.all_gather(jnp.concatenate(new), SEQ_AXIS, axis=1, tiled=True)

        new_down = renew([(w_down, jnp.stack(sums_down))])
        new_up = renew([(w_up, jnp.stack(sums_up))])
        small = [(w_outs, jnp.stack(sums_out))]
        small += [(w_rows[idx], jnp.stack([sums[idx] for sums in sums_qkv])) for idx in range(3)]
        small = renew(small).reshape(4, layers, heads, head_dim, d_model)
        new_down = emit(new_down)
        new_up = emit(new_up)
        new_out = small[0]
        new_heads = [small[idx + 1].transpose(0, 3, 1, 2) for idx in range(3)]
        return (y_out.reshape(x_in.shape), grad_x.reshape(x_in.shape), *new_heads, new_out, new_up, new_down)

    return jax.shard_map(body, mesh=mesh, in_specs=(act_spec, pos_spec, act_spec) + (replicated,) * 9, out_specs=(act_spec, act_spec) + (new_spec,) * 6, check_vma=False)
```

time: 2130 us -> 1170 us (0.55)
  waiting for transfers between devices: 1050 us -> 500 us
  matrix products: 492 us -> 248 us
  other arithmetic: 209 us -> 31.1 us
  Pallas kernels: 0 us -> 163 us
  local copies, waits for them, and re-layouts: 278 us -> 129 us
    psum x1 -> x0, waiting for transfers between devices: 932 us -> none  [body(): lax.psum(tuple((jnp.stack([grads[index] for grads in layer_grads]) for in...]
    all_gather x0 -> x7, waiting for transfers between devices: none -> 282 us  [the longest x3 191 us: renew(): return lax.all_gather(jnp.concatenate(new), SEQ_AXIS, axis=1, tiled=True)]
    dot_general x48 -> x46, matrix products: 492 us -> 248 us  [contract(): return jnp.einsum(form, left, right, preferred_element_type=F32)]
    pallas_call x0 -> x10, Pallas kernels: none -> 163 us  [the longest x4 72.1 us: attn_forward(): pl.pallas_call(functools.partial(attn_fwd_kernel, head_dim, blk), grid=(b...]
    all_to_all x22 -> x0, local copies, waits for them, and re-layouts: 103 us -> none  [the longest x10 62 us: to_seq(): return lax.all_to_all(tensor, SEQ_AXIS, 1, 2, tiled=True)]
    reduce_scatter x0 -> x6, waiting for transfers between devices: none -> 76.9 us  [scatter(): return lax.psum_scatter(grad, SEQ_AXIS, scatter_dimension=0, tiled=True)]
    another operation x10 -> x0, other arithmetic: 76.7 us -> none  [the longest x6 67.8 us: body(): jnp.stack([grads[index] for grads in layer_grads])]
    convert_element_type x10 -> x20, other arithmetic: 77.6 us -> 21.8 us  [the longest x6 13.4 us: renew(): (mine(weight, 1).astype(F32) - learn_rate * total).astype(BF16)]
  transfers between devices with their start and end apart: 17 -> 25, of which waited for: 10 -> 18; matrix products, arithmetic and copies ran while one was open for 16% -> 26% of each run, Pallas kernels for 0% -> 13%
where the time goes in v1:
time: 1170 us; the launch traced here: 1160 us
  waiting for transfers between devices  500 us (43%)
  matrix products  248 us (21%)
  Pallas kernels  163 us (14%)
  local copies, waits for them, and re-layouts  129 us (11%)
  starting transfers between devices  55.7 us (5%)
  other arithmetic  31.1 us (3%)
  blocking collectives  18.3 us (2%)
  between operations  16.7 us (1%)
    dot_general x46, matrix products, contract(): return jnp.einsum(form, left, right, preferred_element_type=F32)  248 us
    all_gather x3, waiting for transfers between devices, renew(): return lax.all_gather(jnp.concatenate(new), SEQ_AXIS, axis=1, tiled=True)  191 us
    all_to_all x12, waiting for transfers between devices, exchange(): return lax.all_to_all(tensor, SEQ_AXIS, 0, 0, tiled=True)  139 us
    all_gather x4, waiting for transfers between devices, body(): n_all = lax.all_gather(norms[c][0].reshape(part, rows, d_model), SEQ_AXIS)  90.8 us
    reduce_scatter x6, waiting for transfers between devices, scatter(): return lax.psum_scatter(grad, SEQ_AXIS, scatter_dimension=0, tiled=True)  76.9 us
    pallas_call x4, Pallas kernels, attn_forward(): pl.pallas_call(functools.partial(attn_fwd_kernel, head_dim, blk), grid=(b...  72.1 us
    pallas_call x4, Pallas kernels, attn_backward(): pl.pallas_call(functools.partial(attn_bwd_kernel, head_dim, blk), grid=(b...  62.7 us
    all_to_all x12, starting transfers between devices, exchange(): return lax.all_to_all(tensor, SEQ_AXIS, 0, 0, tiled=True)  54.3 us
  transfers between devices with their start and end apart: 25, of which 18 were waited for; matrix products, arithmetic and copies ran while one was open for 26% of the time, Pallas kernels for 13%

profile of v1, /device:TPU:112, one launch (start us, length us, event | category | flops | bytes accessed | tf_op | source)
XLA Modules:
  0.0 1162.4 jit_solution(12034628627137412539)
XLA Ops:
  13.0 18.3 %all-gather.2 = s32[8,1,128]{2,1,0:T(1,128)S(1)} all-gather(s32[1,1,128]{2,1,0:T(1,128)S(1)} %bitcast.478), channel_id=1, replica_groups=mesh['dp'=2,'sp'=8] {'sp'}, dimensions={0}, use_global_device_ids=true | all-gather | bytes 4608 | tf_op jit(solution)/shard_map/all_gather | solution.py:244
  41.2 10.8 all-gather.21.cloned.1.call-done
  52.0 18.0 %attn_fwd.4 = (bf16[8,3,128,128]{3,2,1,0:T(8,128)(2,1)S(1)}, bf16[8,3,128,128]{3,2,1,0:T(8,128)(2,1)S(1)}, bf16[8,3,128,128]{3,2,1,0:T(8,128)(2,1)S(1)}, bf16[8,...) custom-call(bf16[8,3,128,1024]{3,2,1,0:T(8,128)(2,1)} %bitcast.393, bf16[384,1024]{1,0:T(8,128)(2,1)} %get-tuple-element.161.w_ref, ...), custom_call_target="tpu_custom_call" | custom-call | flops 16106127360 | bytes 6291456 | tf_op jit(solution)/shard_map/attn_fwd/pallas_call | solution.py:113
  72.7 4.6 all-to-all-start
  77.3 21.1 %all-gather.23.cloned.1.call-done = bf16[24,128,1024]{2,1,0:T(8,128)(2,1)} async-done(((bf16[3,128,1024]{2,1,0:T(8,128)(2,1)}), bf16[24,128,1024]{2,1,0:T(8,128)(2,1)}) %all-gather.23.cloned.1.call-update) | async-done | bytes 6291472 | tf_op jit(solution)/shard_map/all_gather | solution.py:283
  98.4 18.0 %attn_fwd.5 = (bf16[8,3,128,128]{3,2,1,0:T(8,128)(2,1)S(1)}, bf16[8,3,128,128]{3,2,1,0:T(8,128)(2,1)S(1)}, bf16[8,3,128,128]{3,2,1,0:T(8,128)(2,1)S(1)}, bf16[8,...) custom-call(bf16[8,3,128,1024]{3,2,1,0:T(8,128)(2,1)} %bitcast.395, bf16[384,1024]{1,0:T(8,128)(2,1)} %get-tuple-element.161.w_ref, ...), custom_call_target="tpu_custom_call" | custom-call | flops 16106127360 | bytes 6291456 | tf_op jit(solution)/shard_map/attn_fwd/pallas_call | solution.py:113
  128.0 10.8 fusion.67
  151.6 11.3 fusion.83
  169.3 37.7 %all-gather.13.cloned.1.call-done.n_ref = bf16[8,3,128,1024]{3,2,1,0:T(8,128)(2,1)} async-done(((bf16[1,3,128,1024]{3,2,1,0:T(8,128)(2,1)}), bf16[8,3,128,1024]{3,2,1,0:T(8,128)(2,1)}) %all-gather.13.cloned.1.call-update) | async-done | bytes 6291472 | tf_op jit(solution)/shard_map/all_gather | solution.py:283
  207.0 18.0 %attn_fwd.7 = (bf16[8,3,128,128]{3,2,1,0:T(8,128)(2,1)S(1)}, bf16[8,3,128,128]{3,2,1,0:T(8,128)(2,1)S(1)}, bf16[8,3,128,128]{3,2,1,0:T(8,128)(2,1)S(1)}, bf16[8,...) custom-call(bf16[8,3,128,1024]{3,2,1,0:T(8,128)(2,1)} %all-gather.13.cloned.1.call-done.n_ref, ...), custom_call_target="tpu_custom_call" | custom-call | flops 16106127360 | bytes 6291456 | tf_op jit(solution)/shard_map/attn_fwd/pallas_call | solution.py:113
  232.2 21.2 %all-gather.11.cloned.1.call-done.n_ref = bf16[8,3,128,1024]{3,2,1,0:T(8,128)(2,1)} async-done(((bf16[1,3,128,1024]{3,2,1,0:T(8,128)(2,1)}), bf16[8,3,128,1024]{3,2,1,0:T(8,128)(2,1)}) %all-gather.11.cloned.1.call-update) | async-done | bytes 6291472 | tf_op jit(solution)/shard_map/all_gather | solution.py:283
  253.3 18.0 %attn_fwd.6 = (bf16[8,3,128,128]{3,2,1,0:T(8,128)(2,1)S(1)}, bf16[8,3,128,128]{3,2,1,0:T(8,128)(2,1)S(1)}, bf16[8,3,128,128]{3,2,1,0:T(8,128)(2,1)S(1)}, bf16[8,...) custom-call(bf16[8,3,128,1024]{3,2,1,0:T(8,128)(2,1)} %all-gather.11.cloned.1.call-done.n_ref, ...), custom_call_target="tpu_custom_call" | custom-call | flops 16106127360 | bytes 6291456 | tf_op jit(solution)/shard_map/attn_fwd/pallas_call | solution.py:113
  281.0 10.5 all-to-all-done.2
  299.6 11.2 fusion.91
  310.9 6.9 fusion.75
  317.9 12.3 %fusion.92 = f32[4096,1024]{1,0:T(8,128)} fusion(bf16[768,1024]{1,0:T(8,128)(2,1)S(1)} %bitcast.452, bf16[384,4096]{1,0:T(8,128)(2,1)S(1)} %get-tuple-element.203, bf16[384,4096]{1,0:T(8,128)(2,1)} %get-tuple-element.205), kind=kOutput, calls=%fused_computation.104 | convolution fusion | flops 6455033856 | bytes 24641536 | tf_op jit(solution)/shard_map/tf,td->fd/dot_general | solution.py:22
  332.2 11.4 fusion.38
  343.6 10.3 fusion.45
  355.7 10.8 fusion.96
  366.6 8.3 fusion.166
  378.7 4.4 all-to-all-start.4
  383.1 8.3 fusion.193
  395.1 5.6 all-to-all-done.4.d_ref
  400.6 4.6 all-to-all-start.5
  405.3 5.2 fusion.281
  414.3 8.5 all-to-all-done.5.d_ref
  426.2 15.7 %attn_bwd.4 = bf16[8,3,3,128,128]{4,3,2,1,0:T(8,128)(2,1)} custom-call(bf16[8,3,128,128]{3,2,1,0:T(8,128)(2,1)S(1)} %copy-done.13, bf16[8,3,128,128]{3,2,1,0:T(8,128)(2,1)S(1)} %copy-done.15, bf16[8,3,128,128]{3,2,1,0:T(8,128)(2,1)S(1)} %copy-done.17, bf16[8,3,128,128]{3,2,1,0:T(8,128)(2,1)} %get-tuple-element.66.o_ref, ...), custom_call_target="tpu_custom_call" | custom-call | flops 16106127360 | bytes 6291456 | tf_op jit(solution)/shard_map/attn_bwd/pallas_call | solution.py:189
  442.0 4.6 all-to-all-start.6
  446.6 5.4 fusion.283
  458.0 15.6 %attn_bwd.5 = bf16[8,3,3,128,128]{4,3,2,1,0:T(8,128)(2,1)} custom-call(bf16[8,3,128,128]{3,2,1,0:T(8,128)(2,1)S(1)} %copy-done.7, bf16[8,3,128,128]{3,2,1,0:T(8,128)(2,1)S(1)} %copy-done.9, bf16[8,3,128,128]{3,2,1,0:T(8,128)(2,1)S(1)} %copy-done.11, bf16[8,3,128,128]{3,2,1,0:T(8,128)(2,1)} %get-tuple-element.68.o_ref, ...), custom_call_target="tpu_custom_call" | custom-call | flops 16106127360 | bytes 6291456 | tf_op jit(solution)/shard_map/attn_bwd/pallas_call | solution.py:189
  473.6 15.7 %all-to-all-done.6 = bf16[8,3,3,128,128]{4,3,2,1,0:T(8,128)(2,1)} async-done(((bf16[8,3,3,128,128]{4,3,2,1,0:T(8,128)(2,1)}), bf16[8,3,3,128,128]{4,3,2,1,0:T(8,128)(2,1)}, u32[]{:S(2)}, u32[]{:S(2)}) %all-to-all-start.6) | async-done | bytes 2359328 | tf_op jit(solution)/shard_map/all_to_all | solution.py:207
  489.3 4.8 all-to-all-start.7
  494.3 5.8 fusion.108
  500.1 6.7 bitcast_add_fusion.1
  506.7 30.2 %all-to-all-done.7 = bf16[8,3,3,128,128]{4,3,2,1,0:T(8,128)(2,1)} async-done(((bf16[8,3,3,128,128]{4,3,2,1,0:T(8,128)(2,1)}), bf16[8,3,3,128,128]{4,3,2,1,0:T(8,128)(2,1)}, u32[]{:S(2)}, u32[]{:S(2)}) %all-to-all-start.7) | async-done | bytes 2359328 | tf_op jit(solution)/shard_map/all_to_all | solution.py:207
  571.5 10.8 fusion.100
  582.4 10.2 fusion.52
  592.7 11.3 fusion.59
  605.7 10.6 fusion.104
  617.0 8.2 fusion.148
  633.4 8.3 fusion.175
  645.3 5.5 all-to-all-done.8.d_ref
  650.9 4.6 all-to-all-start.9
  655.5 5.7 fusion.210
  661.2 11.9 %all-to-all-done.9.d_ref = bf16[8,3,128,128]{3,2,1,0:T(8,128)(2,1)} async-done(((bf16[8,3,128,128]{3,2,1,0:T(8,128)(2,1)}), bf16[8,3,128,128]{3,2,1,0:T(8,128)(2,1)}, u32[]{:S(2)}, u32[]{:S(2)}) %all-to-all-start.9) | async-done | bytes 786464 | tf_op jit(solution)/shard_map/all_to_all | solution.py:207
  676.7 15.7 %attn_bwd.6 = bf16[8,3,3,128,128]{4,3,2,1,0:T(8,128)(2,1)} custom-call(bf16[8,3,128,128]{3,2,1,0:T(8,128)(2,1)S(1)} %copy-done.1, bf16[8,3,128,128]{3,2,1,0:T(8,128)(2,1)S(1)} %copy-done.3, bf16[8,3,128,128]{3,2,1,0:T(8,128)(2,1)S(1)} %copy-done.5, bf16[8,3,128,128]{3,2,1,0:T(8,128)(2,1)} %get-tuple-element.63.o_ref, ...), custom_call_target="tpu_custom_call" | custom-call | flops 16106127360 | bytes 6291456 | tf_op jit(solution)/shard_map/attn_bwd/pallas_call | solution.py:189
  692.3 4.6 all-to-all-start.10
  698.3 15.7 %attn_bwd.7 = bf16[8,3,3,128,128]{4,3,2,1,0:T(8,128)(2,1)} custom-call(bf16[8,3,128,128]{3,2,1,0:T(8,128)(2,1)S(1)} %get-tuple-element.98.q_ref, bf16[8,3,128,128]{3,2,1,0:T(8,128)(2,1)S(1)} %get-tuple-element.99.k_ref, bf16[8,3,128,128]{3,2,1,0:T(8,128)(2,1)S(1)} %get-tuple-element.100.v_ref, bf16[8,3,128,128]{3,2,1,0:T(8,128)(2,1)} %get-tuple-element.64.o_ref, ...), custom_call_target="tpu_custom_call" | custom-call | flops 16106127360 | bytes 6291456 | tf_op jit(solution)/shard_map/attn_bwd/pallas_call | solution.py:189
  713.9 25.8 %all-to-all-done.10 = bf16[8,3,3,128,128]{4,3,2,1,0:T(8,128)(2,1)} async-done(((bf16[8,3,3,128,128]{4,3,2,1,0:T(8,128)(2,1)}), bf16[8,3,3,128,128]{4,3,2,1,0:T(8,128)(2,1)}, u32[]{:S(2)}, u32[]{:S(2)}) %all-to-all-start.10) | async-done | bytes 2359328 | tf_op jit(solution)/shard_map/all_to_all | solution.py:207
  739.7 4.6 all-to-all-start.11
  747.1 5.7 fusion.299
  752.9 6.6 bitcast_add_fusion
  759.4 25.7 %all-to-all-done.11 = bf16[8,3,3,128,128]{4,3,2,1,0:T(8,128)(2,1)} async-done(((bf16[8,3,3,128,128]{4,3,2,1,0:T(8,128)(2,1)}), bf16[8,3,3,128,128]{4,3,2,1,0:T(8,128)(2,1)}, u32[]{:S(2)}, u32[]{:S(2)}) %all-to-all-start.11) | async-done | bytes 2359328 | tf_op jit(solution)/shard_map/all_to_all | solution.py:207
  811.8 42.1 %reduce-scatter.15.cloned.1.call-done = f32[128,4096]{1,0:T(8,128)} async-done(((f32[1024,4096]{1,0:T(8,128)}), f32[128,4096]{1,0:T(8,128)}) %reduce-scatter.15.cloned.1.call-update) | async-done | bytes 2097168 | tf_op jit(solution)/shard_map/reduce_scatter | solution.py:275
  855.1 34.8 %reduce-scatter.17.cloned.1.call-done = f32[128,1024]{1,0:T(8,128)} async-done(((f32[1024,1024]{1,0:T(8,128)}), f32[128,1024]{1,0:T(8,128)}) %reduce-scatter.17.cloned.1.call-update) | async-done | bytes 524304 | tf_op jit(solution)/shard_map/reduce_scatter | solution.py:275
  902.4 5.2 fusion.131
  907.8 7.9 fusion.188
  915.7 6.0 fusion.161
  922.9 52.5 %all-gather.15.cloned.1.call-done = bf16[8,1024,1024]{2,1,0:T(8,128)(2,1)} async-done(((bf16[8,128,1024]{2,1,0:T(8,128)(2,1)}), bf16[8,1024,1024]{2,1,0:T(8,128)(2,1)}) %all-gather.15.cloned.1.call-update) | async-done | bytes 16777232 | tf_op jit(solution)/shard_map/all_gather | solution.py:351
  975.4 13.4 %fusion.280 = (bf16[2,1024,1024]{2,1,0:T(8,128)(2,1)}, bf16[2,1024,1024]{2,1,0:T(8,128)(2,1)}, bf16[2,1024,1024]{2,1,0:T(8,128)(2,1)}, bf16[2,1024,1024]{2,1,0:T(8,128)(2,1)}) fusion(bf16[8,1024,1024]{2,1,0:T(8,128)(2,1)} %all-gather.15.cloned.1.call-done), kind=kLoop, calls=%fused_computation.363 | loop fusion | bytes 33554432 | tf_op jit(solution)/shard_map/slice | solution.py:360
  988.8 70.0 %all-gather.17.cloned.1.call-done.in_ref = bf16[2,1024,4096]{2,1,0:T(8,128)(2,1)} async-done(((bf16[2,128,4096]{2,1,0:T(8,128)(2,1)}), bf16[2,1024,4096]{2,1,0:T(8,128)(2,1)}) %all-gather.17.cloned.1.call-update) | async-done | bytes 16777232 | tf_op jit(solution)/shard_map/all_gather | solution.py:351
  1058.8 14.5 %emit.2 = bf16[2,1024,4096]{2,1,0:T(8,128)(2,1)} custom-call(bf16[2,1024,4096]{2,1,0:T(8,128)(2,1)} %all-gather.17.cloned.1.call-done.in_ref), custom_call_target="tpu_custom_call" | custom-call | flops 10000000000 | bytes 33554432 | tf_op jit(solution)/shard_map/emit/pallas_call | solution.py:217
  1073.4 68.5 %all-gather.19.cloned.1.call-done.in_ref = bf16[2,4096,1024]{2,1,0:T(8,128)(2,1)} async-done(((bf16[2,512,1024]{2,1,0:T(8,128)(2,1)}), bf16[2,4096,1024]{2,1,0:T(8,128)(2,1)}) %all-gather.19.cloned.1.call-update) | async-done | bytes 16777232 | tf_op jit(solution)/shard_map/all_gather | solution.py:351
  1141.8 13.8 %emit.3 = bf16[2,4096,1024]{2,1,0:T(8,128)(2,1)} custom-call(bf16[2,4096,1024]{2,1,0:T(8,128)(2,1)} %all-gather.19.cloned.1.call-done.in_ref), custom_call_target="tpu_custom_call" | custom-call | flops 10000000000 | bytes 33554432 | tf_op jit(solution)/shard_map/emit/pallas_call | solution.py:217
  (456 shorter events, 194.9 us)
Async XLA Ops:
  7.2 44.8 %all-gather.21.cloned.1.call-start = ((), (), s32[]{:S(2)}) async-start(), calls=%async_computation.29 | async-start | bytes 7077888 | tf_op jit(solution)/shard_map/all_gather | solution.py:283
  9.9 157.3 %copy-start.110 = (f32[1,1024]{1,0:T(1,128)}, f32[1,1024]{1,0:T(1,128)S(1)}, u32[]{:S(2)}) copy-start(f32[1,1024]{1,0:T(1,128)S(1)} %get-tuple-element.166) | copy-start | bytes 12292
  12.2 86.2 %all-gather.23.cloned.1.call-start = ((), (), s32[]{:S(2)}) async-start(), calls=%async_computation.30 | async-start | bytes 7077888 | tf_op jit(solution)/shard_map/all_gather | solution.py:283
  35.0 115.7 %copy-start.114 = (f32[1,1024]{1,0:T(1,128)}, f32[1,1024]{1,0:T(1,128)S(1)}, u32[]{:S(2)}) copy-start(f32[1,1024]{1,0:T(1,128)S(1)} %get-tuple-element.165) | copy-start | bytes 12292
  72.7 43.7 %all-to-all-start = ((bf16[8,3,128,128]{3,2,1,0:T(8,128)(2,1)}), bf16[8,3,128,128]{3,2,1,0:T(8,128)(2,1)}, u32[]{:S(2)}, u32[]{:S(2)}) async-start(bf16[8,3,128,128]{3,2,1,0:T(8,128)(2,1)} %get-tuple-element.63.o_ref), calls=%async_computation | async-start | bytes 1572864 | tf_op jit(solution)/shard_map/all_to_all | solution.py:207
  116.4 28.1 %all-to-all-start.1 = ((bf16[8,3,128,128]{3,2,1,0:T(8,128)(2,1)}), bf16[8,3,128,128]{3,2,1,0:T(8,128)(2,1)}, u32[]{:S(2)}, u32[]{:S(2)}) async-start(bf16[8,3,128,128]{3,2,1,0:T(8,128)(2,1)} %get-tuple-element.64.o_ref), calls=%async_computation.1 | async-start | bytes 1572864 | tf_op jit(solution)/shard_map/all_to_all | solution.py:207
  120.8 86.2 %all-gather.13.cloned.1.call-start = ((), (), s32[]{:S(2)}) async-start(), calls=%async_computation.19 | async-start | bytes 7077888 | tf_op jit(solution)/shard_map/all_gather | solution.py:283
  123.2 15.6 %slice-start.4 = ((s8[16777216]{0:T(1024)(128)(4,1)}), s8[4194304]{0:T(1024)(128)(4,1)S(1)}, s32[]{:S(2)}) async-start(s8[16777216]{0:T(1024)(128)(4,1)} %bitcast.459), calls=%async_computation.35 | async-start | bytes 8388608
  126.5 12.3 %copy-start.46 = (bf16[384,1024]{1,0:T(8,128)(2,1)}, bf16[384,1024]{1,0:T(8,128)(2,1)S(1)}, u32[]{:S(2)}) copy-start(bf16[384,1024]{1,0:T(8,128)(2,1)S(1)} %get-tuple-element.188) | copy-start | bytes 2359300
  127.9 10.9 copy-start.60
  127.9 10.9 slice-start.5
  128.0 10.9 slice-start.6
  128.0 10.9 slice-start.7
  146.8 16.1 %slice-start.8 = ((s8[16777216]{0:T(1024)(128)(4,1)}), s8[4194304]{0:T(1024)(128)(4,1)S(1)}, s32[]{:S(2)}) async-start(s8[16777216]{0:T(1024)(128)(4,1)} %bitcast.461), calls=%async_computation.39 | async-start | bytes 8388608
  150.1 12.9 %copy-start.48 = (bf16[384,1024]{1,0:T(8,128)(2,1)}, bf16[384,1024]{1,0:T(8,128)(2,1)S(1)}, u32[]{:S(2)}) copy-start(bf16[384,1024]{1,0:T(8,128)(2,1)S(1)} %get-tuple-element.194) | copy-start | bytes 2359300
  151.5 11.4 copy-start.62
  151.6 11.4 slice-start.9
  151.6 11.4 slice-start.10
  151.6 11.4 slice-start.11
  168.6 84.7 %all-gather.11.cloned.1.call-start = ((), (), s32[]{:S(2)}) async-start(), calls=%async_computation.18 | async-start | bytes 7077888 | tf_op jit(solution)/shard_map/all_gather | solution.py:283
  227.8 46.3 %all-to-all-start.3 = ((bf16[8,3,128,128]{3,2,1,0:T(8,128)(2,1)}), bf16[8,3,128,128]{3,2,1,0:T(8,128)(2,1)}, u32[]{:S(2)}, u32[]{:S(2)}) async-start(bf16[8,3,128,128]{3,2,1,0:T(8,128)(2,1)} %get-tuple-element.68.o_ref), calls=%async_computation.3 | async-start | bytes 1572864 | tf_op jit(solution)/shard_map/all_to_all | solution.py:207
  274.0 17.4 %all-to-all-start.2 = ((bf16[8,3,128,128]{3,2,1,0:T(8,128)(2,1)}), bf16[8,3,128,128]{3,2,1,0:T(8,128)(2,1)}, u32[]{:S(2)}, u32[]{:S(2)}) async-start(bf16[8,3,128,128]{3,2,1,0:T(8,128)(2,1)} %get-tuple-element.66.o_ref), calls=%async_computation.2 | async-start | bytes 1572864 | tf_op jit(solution)/shard_map/all_to_all | solution.py:207
  278.4 258.5 %reduce-scatter.7.cloned.1.call-start = ((), (), s32[]{:S(2)}) async-start(), calls=%async_computation.20 | async-start | bytes 18874368 | tf_op jit(solution)/shard_map/reduce_scatter | solution.py:275
  297.1 13.8 %slice-start = ((s8[16777216]{0:T(1024)(128)(4,1)}), s8[4194304]{0:T(1024)(128)(4,1)S(1)}, s32[]{:S(2)}) async-start(s8[16777216]{0:T(1024)(128)(4,1)} %bitcast.457), calls=%async_computation.31 | async-start | bytes 8388608
  299.6 11.3 copy-start.66
  299.6 11.3 copy-start.64
  299.6 11.3 slice-start.1
  299.6 11.3 slice-start.2
  299.6 11.3 slice-start.3
  330.2 286.1 %reduce-scatter.9.cloned.1.call-start = ((), (), s32[]{:S(2)}) async-start(), calls=%async_computation.21 | async-start | bytes 18874368 | tf_op jit(solution)/shard_map/reduce_scatter | solution.py:275
  330.5 13.1 %slice-start.12 = ((s8[6291456]{0:T(1024)(128)(4,1)}), s8[4194304]{0:T(1024)(128)(4,1)S(1)}, s32[]{:S(2)}) async-start(s8[6291456]{0:T(1024)(128)(4,1)} %bitcast.479), calls=%async_computation.43 | async-start | bytes 8388608
  332.1 11.4 copy-start.90
  332.1 11.4 copy-start.88
  332.2 11.4 slice-start.13
  343.6 10.4 copy-start.71
  343.6 12.1 %copy-start.65 = (bf16[384,1024]{1,0:T(8,128)(2,1)S(1)}, bf16[384,1024]{1,0:T(8,128)(2,1)}, u32[]{:S(2)}) copy-start(bf16[384,1024]{1,0:T(8,128)(2,1)} %copy-done.64) | copy-start | bytes 2359300
  343.6 12.0 %copy-start.67 = (bf16[384,1024]{1,0:T(8,128)(2,1)S(1)}, bf16[384,1024]{1,0:T(8,128)(2,1)}, u32[]{:S(2)}) copy-start(bf16[384,1024]{1,0:T(8,128)(2,1)} %copy-done.66) | copy-start | bytes 2359300
  378.7 22.0 %all-to-all-start.4 = ((bf16[8,3,128,128]{3,2,1,0:T(8,128)(2,1)}), bf16[8,3,128,128]{3,2,1,0:T(8,128)(2,1)}, u32[]{:S(2)}, u32[]{:S(2)}) async-start(bf16[8,3,128,128]{3,2,1,0:T(8,128)(2,1)} %bitcast.424), calls=%async_computation.4 | async-start | bytes 1572864 | tf_op jit(solution)/shard_map/all_to_all | solution.py:207
  400.6 22.2 %all-to-all-start.5 = ((bf16[8,3,128,128]{3,2,1,0:T(8,128)(2,1)}), bf16[8,3,128,128]{3,2,1,0:T(8,128)(2,1)}, u32[]{:S(2)}, u32[]{:S(2)}) async-start(bf16[8,3,128,128]{3,2,1,0:T(8,128)(2,1)} %bitcast.426), calls=%async_computation.5 | async-start | bytes 1572864 | tf_op jit(solution)/shard_map/all_to_all | solution.py:207
  442.0 47.4 %all-to-all-start.6 = ((bf16[8,3,3,128,128]{4,3,2,1,0:T(8,128)(2,1)}), bf16[8,3,3,128,128]{4,3,2,1,0:T(8,128)(2,1)}, u32[]{:S(2)}, u32[]{:S(2)}) async-start(bf16[8,3,3,128,128]{4,3,2,1,0:T(8,128)(2,1)} %attn_bwd.4), calls=%async_computation.6 | async-start | bytes 4718592 | tf_op jit(solution)/shard_map/all_to_all | solution.py:207
  446.5 214.6 %reduce-scatter.11.cloned.1.call-start = ((), (), s32[]{:S(2)}) async-start(), calls=%async_computation.22 | async-start | bytes 4718592 | tf_op jit(solution)/shard_map/reduce_scatter | solution.py:275
  473.6 20.6 %copy-start.132 = (f32[384,1]{0,1:T(1,128)S(1)}, f32[384,1]{0,1:T(1,128)}, u32[]{:S(2)}) copy-start(f32[384,1]{0,1:T(1,128)} %rsqrt.103) | copy-start | bytes 4612
  489.3 47.6 %all-to-all-start.7 = ((bf16[8,3,3,128,128]{4,3,2,1,0:T(8,128)(2,1)}), bf16[8,3,3,128,128]{4,3,2,1,0:T(8,128)(2,1)}, u32[]{:S(2)}, u32[]{:S(2)}) async-start(bf16[8,3,3,128,128]{4,3,2,1,0:T(8,128)(2,1)} %attn_bwd.5), calls=%async_computation.7 | async-start | bytes 4718592 | tf_op jit(solution)/shard_map/all_to_all | solution.py:207
  494.1 291.0 %reduce-scatter.13.cloned.1.call-start = ((), (), s32[]{:S(2)}) async-start(), calls=%async_computation.23 | async-start | bytes 18874368 | tf_op jit(solution)/shard_map/reduce_scatter | solution.py:275
  582.4 271.5 %reduce-scatter.15.cloned.1.call-start = ((), (), s32[]{:S(2)}) async-start(), calls=%async_computation.24 | async-start | bytes 18874368 | tf_op jit(solution)/shard_map/reduce_scatter | solution.py:275
  582.4 10.2 copy-start.84
  592.7 11.3 copy-start.70
  592.7 13.0 %copy-start.61 = (bf16[384,1024]{1,0:T(8,128)(2,1)S(1)}, bf16[384,1024]{1,0:T(8,128)(2,1)}, u32[]{:S(2)}) copy-start(bf16[384,1024]{1,0:T(8,128)(2,1)} %copy-done.60) | copy-start | bytes 2359300
  592.7 13.0 %copy-start.63 = (bf16[384,1024]{1,0:T(8,128)(2,1)S(1)}, bf16[384,1024]{1,0:T(8,128)(2,1)}, u32[]{:S(2)}) copy-start(bf16[384,1024]{1,0:T(8,128)(2,1)} %copy-done.62) | copy-start | bytes 2359300
  628.9 21.9 %all-to-all-start.8 = ((bf16[8,3,128,128]{3,2,1,0:T(8,128)(2,1)}), bf16[8,3,128,128]{3,2,1,0:T(8,128)(2,1)}, u32[]{:S(2)}, u32[]{:S(2)}) async-start(bf16[8,3,128,128]{3,2,1,0:T(8,128)(2,1)} %bitcast.423), calls=%async_computation.10 | async-start | bytes 1572864 | tf_op jit(solution)/shard_map/all_to_all | solution.py:207
  650.9 22.2 %all-to-all-start.9 = ((bf16[8,3,128,128]{3,2,1,0:T(8,128)(2,1)}), bf16[8,3,128,128]{3,2,1,0:T(8,128)(2,1)}, u32[]{:S(2)}, u32[]{:S(2)}) async-start(bf16[8,3,128,128]{3,2,1,0:T(8,128)(2,1)} %bitcast.425), calls=%async_computation.11 | async-start | bytes 1572864 | tf_op jit(solution)/shard_map/all_to_all | solution.py:207
  692.3 47.4 %all-to-all-start.10 = ((bf16[8,3,3,128,128]{4,3,2,1,0:T(8,128)(2,1)}), bf16[8,3,3,128,128]{4,3,2,1,0:T(8,128)(2,1)}, u32[]{:S(2)}, u32[]{:S(2)}) async-start(bf16[8,3,3,128,128]{4,3,2,1,0:T(8,128)(2,1)} %attn_bwd.6), calls=%async_computation.13 | async-start | bytes 4718592 | tf_op jit(solution)/shard_map/all_to_all | solution.py:207
  696.9 192.9 %reduce-scatter.17.cloned.1.call-start = ((), (), s32[]{:S(2)}) async-start(), calls=%async_computation.25 | async-start | bytes 4718592 | tf_op jit(solution)/shard_map/reduce_scatter | solution.py:275
  739.7 45.4 %all-to-all-start.11 = ((bf16[8,3,3,128,128]{4,3,2,1,0:T(8,128)(2,1)}), bf16[8,3,3,128,128]{4,3,2,1,0:T(8,128)(2,1)}, u32[]{:S(2)}, u32[]{:S(2)}) async-start(bf16[8,3,3,128,128]{4,3,2,1,0:T(8,128)(2,1)} %attn_bwd.7), calls=%async_computation.14 | async-start | bytes 4718592 | tf_op jit(solution)/shard_map/all_to_all | solution.py:207
  744.3 231.1 %all-gather.15.cloned.1.call-start = ((), (), s32[]{:S(2)}) async-start(), calls=%async_computation.26 | async-start | bytes 18874368 | tf_op jit(solution)/shard_map/all_gather | solution.py:351
  810.5 43.4 %copy-start.50 = (f32[3,128,1024]{2,1,0:T(8,128)S(1)}, f32[3,128,1024]{2,1,0:T(8,128)}, u32[]{:S(2)}) copy-start(f32[3,128,1024]{2,1,0:T(8,128)} %bitcast_add_fusion) | copy-start | bytes 4718596
  811.8 78.1 %copy-start.56 = (bf16[2,128,1024]{2,1,0:T(8,128)(2,1)S(1)}, bf16[2,128,1024]{2,1,0:T(8,128)(2,1)}, u32[]{:S(2)}) copy-start(bf16[2,128,1024]{2,1,0:T(8,128)(2,1)} %copy-done.55) | copy-start | bytes 1572868
  811.8 79.5 %copy-start.54 = (bf16[2,128,1024]{2,1,0:T(8,128)(2,1)S(1)}, bf16[2,128,1024]{2,1,0:T(8,128)(2,1)}, u32[]{:S(2)}) copy-start(bf16[2,128,1024]{2,1,0:T(8,128)(2,1)} %copy-done.53) | copy-start | bytes 1572868
  811.8 79.5 %copy-start.103 = (f32[1,128,1024]{2,1,0:T(8,128)S(1)}, f32[1,128,1024]{2,1,0:T(8,128)}, u32[]{:S(2)}) copy-start(f32[1,128,1024]{2,1,0:T(8,128)} %get-tuple-element.155) | copy-start | bytes 1572868
  855.1 36.2 %copy-start.104 = (f32[1,128,1024]{2,1,0:T(8,128)S(1)}, f32[1,128,1024]{2,1,0:T(8,128)}, u32[]{:S(2)}) copy-start(f32[1,128,1024]{2,1,0:T(8,128)} %get-tuple-element.152) | copy-start | bytes 1572868
  855.1 36.4 %copy-start.105 = (f32[1,128,1024]{2,1,0:T(8,128)S(1)}, f32[1,128,1024]{2,1,0:T(8,128)}, u32[]{:S(2)}) copy-start(f32[1,128,1024]{2,1,0:T(8,128)} %get-tuple-element.153) | copy-start | bytes 1572868
  855.1 36.4 %copy-start.106 = (f32[1,128,1024]{2,1,0:T(8,128)S(1)}, f32[1,128,1024]{2,1,0:T(8,128)}, u32[]{:S(2)}) copy-start(f32[1,128,1024]{2,1,0:T(8,128)} %get-tuple-element.150) | copy-start | bytes 1572868
  895.6 163.2 %all-gather.17.cloned.1.call-start = ((), (), s32[]{:S(2)}) async-start(), calls=%async_computation.27 | async-start | bytes 18874368 | tf_op jit(solution)/shard_map/all_gather | solution.py:351
  900.5 241.3 %all-gather.19.cloned.1.call-start = ((), (), s32[]{:S(2)}) async-start(), calls=%async_computation.28 | async-start | bytes 18874368 | tf_op jit(solution)/shard_map/all_gather | solution.py:351
  (115 other events, 332.5 us)
Sparse Core Ops, SparseCore 0:
  12.3 39.6 all-gather.20
  54.1 44.2 all-gather.22
  168.8 38.2 all-gather.12
  209.0 44.2 all-gather.10
  330.3 103.9 reduce-scatter.6
  437.1 137.8 reduce-scatter.8
  577.8 33.4 reduce-scatter.10
  613.6 128.6 reduce-scatter.12
  745.3 108.5 reduce-scatter.14
  856.6 33.2 reduce-scatter.16
  895.7 79.6 all-gather.14
  977.4 81.3 all-gather.16
  1060.4 81.3 all-gather.18

commit v2 on v1

--- a/solution.py
+++ b/solution.py
@@ -12,6 +12,7 @@
 EPSILON = 1e-5
 ROPE_BASE = 10000.0
 SEQ_AXIS = 'sp'
+CORES = 2
 F32 = jnp.float32
 BF16 = jnp.bfloat16
 LOG2E = math.log2(math.e)
@@ -207,24 +208,6 @@
     return lax.all_to_all(tensor, SEQ_AXIS, 0, 0, tiled=True)
 
 
-def emit_kernel(in_ref, out_ref):
-    out_ref[...] = in_ref[...]
-
-
-def emit(array):
-    layers, height, width = array.shape
-    block = pl.BlockSpec((1, max(height // 4, 8), width), lambda layer, row: (layer, row, 0))
-    return pl.pallas_call(
-        emit_kernel,
-        grid=(layers, height // max(height // 4, 8)),
-        in_specs=[block],
-        out_specs=block,
-        out_shape=jax.ShapeDtypeStruct(array.shape, array.dtype),
-        cost_estimate=pl.CostEstimate(flops=10 ** 10, bytes_accessed=4 * array.size, transcendentals=0),
-        name='emit',
-    )(array)
-
-
 def solution(mesh):
     act_spec = P('dp', 'sp', None)
     pos_spec = P(('dp', 'sp'))
@@ -271,8 +254,24 @@
         def to_tokens(heads_first):
             return heads_first.reshape(shards, size, lanes).transpose(1, 0, 2).reshape(size, heads * head_dim)
 
-        def scatter(grad):
-            return lax.psum_scatter(grad, SEQ_AXIS, scatter_dimension=0, tiled=True)
+        chips = shards // CORES
+        rings = [[chip * CORES + c for chip in range(chips)] for c in range(CORES)]
+        swap = [(index, index ^ 1) for index in range(shards)]
+        core = me % CORES
+
+        def side(left, which):
+            width = left.shape[1] // shards
+            pick = [jnp.concatenate([left[:, (chip * CORES + c) * width:(chip * CORES + c + 1) * width] for chip in range(chips)], axis=1) for c in range(CORES)]
+            return jnp.where(which == 0, pick[0], pick[1])
+
+        def send_half(left, right):
+            return contract('tf,td->fd', side(left, 1 - core), right)
+
+        def keep_half(left, right, sent):
+            return contract('tf,td->fd', side(left, core), right) + lax.ppermute(sent, SEQ_AXIS, swap)
+
+        def scatter(grad, paired):
+            return lax.psum_scatter(grad, SEQ_AXIS, scatter_dimension=0, axis_index_groups=rings if paired else None, tiled=True)
 
         acts = split(x_in)
         stash = []
@@ -306,19 +305,30 @@
             saved = stash[layer]
             above = layer + 1 if layer + 1 < layers else None
             whole = d_out.reshape(tokens, d_model) if above is None else join(grads)
-            grad_down = contract('tf,td->fd', join([s[13] for s in saved]), whole)
-            pre_acts, grad_down = order(([s[12] for s in saved], grad_down))
-            sums_down[layer] = scatter(grad_down)
+            paired = above is not None
+            gelu_all, norm_all, mixed_all = (join([item[index] for item in saved]) for index in (13, 10, 8))
+            pre_acts = [item[12] for item in saved]
+            if paired:
+                down_half = send_half(gelu_all, whole)
+                pre_acts, down_half = order((pre_acts, down_half))
+            else:
+                grad_down = contract('tf,td->fd', gelu_all, whole)
+                pre_acts, grad_down = order((pre_acts, grad_down))
             d_pres = []
             for c in range(chunks):
                 d_gelu = contract('td,fd->tf', grads[c], w_down[layer])
                 d_pres.append(jax.vjp(gelu_tanh, pre_acts[c])[1](d_gelu)[0].astype(BF16))
-            grad_up = contract('td,tf->df', join([s[10] for s in saved]), join(d_pres))
-            if above is not None:
-                d_pres, grad_up, sums_up[above] = order((d_pres, grad_up, sums_up[above]))
+            if paired:
+                grad_down = keep_half(gelu_all, whole, down_half)
+                d_pres, grad_down = order((d_pres, grad_down))
+            sums_down[layer] = scatter(grad_down, paired)
+            d_pre_all = join(d_pres)
+            if paired:
+                up_half = send_half(norm_all, d_pre_all)
+                d_pres, up_half, sums_up[above] = order((d_pres, up_half, sums_up[above]))
             else:
+                grad_up = contract('td,tf->df', norm_all, d_pre_all)
                 d_pres, grad_up = order((d_pres, grad_up))
-            sums_up[layer] = scatter(grad_up)
             d_hiddens, d_heads = [], []
             for c in range(chunks):
                 d_norm_mlp = contract('tf,df->td', d_pres[c], w_up[layer])
@@ -326,39 +336,66 @@
                 d_mixed = contract('td,cd->tc', d_hidden, w_outs[layer]).astype(BF16)
                 d_hiddens.append(d_hidden)
                 d_heads.append(exchange(d_mixed.reshape(size, shards, lanes).transpose(1, 0, 2).reshape(shards, part, rows, lanes)))
-            grad_out = contract('tc,td->cd', join([s[8] for s in saved]), join(d_hiddens))
-            if above is not None:
-                d_heads, grad_out, sums_out[above] = order((d_heads, grad_out, sums_out[above]))
+            d_hidden_all = join(d_hiddens)
+            if paired:
+                grad_up = keep_half(norm_all, d_pre_all, up_half)
+                out_half = send_half(mixed_all, d_hidden_all)
+                d_heads, grad_up, out_half, sums_out[above] = order((d_heads, grad_up, out_half, sums_out[above]))
             else:
+                grad_out = contract('tc,td->cd', mixed_all, d_hidden_all)
                 d_heads, grad_out = order((d_heads, grad_out))
-            sums_out[layer] = scatter(grad_out)
+                sums_out[layer] = scatter(grad_out, paired)
+            sums_up[layer] = scatter(grad_up, paired)
             grad_qkv, outs = 0.0, []
             for c in range(chunks):
                 _, n_all, _, q, k, v, o, lse = saved[c][:8]
                 dqkv = attn_backward(q, k, v, o, d_heads[c], lse, cos, sin, head_dim)
                 outs.append(exchange(dqkv))
                 grad_qkv = grad_qkv + contract('sibrc,sbrd->icd', dqkv, n_all)
-            outs, sums_qkv[layer], sums_down[layer] = order((outs, grad_qkv, sums_down[layer]))
+            if paired:
+                sums_out[layer] = scatter(keep_half(mixed_all, d_hidden_all, out_half), paired)
+            if paired:
+                outs, sums_qkv[layer], sums_down[layer], sums_up[layer] = order((outs, grad_qkv, sums_down[layer], sums_up[layer]))
+            else:
+                outs, sums_qkv[layer], sums_down[layer] = order((outs, grad_qkv, sums_down[layer]))
             for c in range(chunks):
                 d_norm_attn = sum(contract('tc,cd->td', to_tokens(outs[c][:, idx]), w_rows[idx][layer]) for idx in range(3))
                 grads[c] = (d_hiddens[c].astype(F32) + rms_norm_grad(saved[c][0], saved[c][2], g_attn[layer], d_norm_attn)).astype(BF16)
         grad_x = join(grads)
-        grad_x, sums_up[0] = order((grad_x, sums_up[0]))
-        sums_up[0], sums_out[0] = order((sums_up[0], sums_out[0]))
-
-        def renew(pairs):
-            new = [(mine(weight, 1).astype(F32) - learn_rate * total).astype(BF16) for weight, total in pairs]
-            return lax.all_gather(jnp.concatenate(new), SEQ_AXIS, axis=1, tiled=True)
-
-        new_down = renew([(w_down, jnp.stack(sums_down))])
-        new_up = renew([(w_up, jnp.stack(sums_up))])
-        small = [(w_outs, jnp.stack(sums_out))]
-        small += [(w_rows[idx], jnp.stack([sums[idx] for sums in sums_qkv])) for idx in range(3)]
-        small = renew(small).reshape(4, layers, heads, head_dim, d_model)
-        new_down = emit(new_down)
-        new_up = emit(new_up)
-        new_out = small[0]
-        new_heads = [small[idx + 1].transpose(0, 3, 1, 2) for idx in range(3)]
+        grad_x, sums_out[0] = order((grad_x, sums_out[0]))
+
+        chip = me // CORES
+        onward = [(index, (index + CORES) % shards) for index in range(shards)]
+        backward = [(index, (index - CORES) % shards) for index in range(shards)]
+        assert chips == 4, chips
+
+        def spread(new):
+            rows_each = new.shape[1]
+            half = rows_each // 2
+            below = lax.ppermute(new, SEQ_AXIS, onward)
+            above = lax.ppermute(new, SEQ_AXIS, backward)
+            far_low = lax.ppermute(below[:, :half], SEQ_AXIS, onward)
+            far_high = lax.ppermute(above[:, half:], SEQ_AXIS, backward)
+            near = [(new, 0, 0), (below, 3, 0), (above, 1, 0)]
+            far = [(far_low, 2, 0), (far_high, 2, half)]
+            pieces = [(piece, lax.ppermute(piece, SEQ_AXIS, swap), hops, low) for piece, hops, low in near]
+            pieces += [(piece, lax.ppermute(piece, SEQ_AXIS, swap), hops, low) for piece, hops, low in far]
+            whole = jnp.zeros((new.shape[0], shards * rows_each, new.shape[2]), new.dtype)
+            for piece, twin, hops, low in pieces:
+                base = (chip + hops) % chips * CORES
+                whole = lax.dynamic_update_slice_in_dim(whole, piece, (base + core) * rows_each + low, 1)
+                whole = lax.dynamic_update_slice_in_dim(whole, twin, (base + 1 - core) * rows_each + low, 1)
+            return whole
+
+        def renew(weight, total):
+            return spread((mine(weight, 1).astype(F32) - learn_rate * total).astype(BF16))
+
+        new_down = renew(w_down, jnp.stack(sums_down))
+        new_up = renew(w_up, jnp.stack(sums_up))
+        new_out = renew(w_outs, jnp.stack(sums_out)).reshape(w_attn_out.shape)
+        new_heads = [
+            renew(w_rows[idx], jnp.stack([sums[idx] for sums in sums_qkv])).reshape(layers, heads, head_dim, d_model).transpose(0, 3, 1, 2)
+            for idx in range(3)]
         return (y_out.reshape(x_in.shape), grad_x.reshape(x_in.shape), *new_heads, new_out, new_up, new_down)
 
     return jax.shard_map(body, mesh=mesh, in_specs=(act_spec, pos_spec, act_spec) + (replicated,) * 9, out_specs=(act_spec, act_spec) + (new_spec,) * 6, check_vma=False)

time: 1170 us -> 1180 us (level)
  waiting for transfers between devices: 500 us -> 400 us
  local copies, waits for them, and re-layouts: 129 us -> 195 us
  starting transfers between devices: 55.7 us -> 97.5 us
  Pallas kernels: 163 us -> 135 us
  matrix products: 248 us -> 268 us
    all_gather x3 -> x0, waiting for transfers between devices: 191 us -> none  [renew(): return lax.all_gather(jnp.concatenate(new), SEQ_AXIS, axis=1, tiled=True)]
    ppermute x0 -> x57, waiting for transfers between devices: none -> 138 us  [the longest x6 74.4 us: spread(): below = lax.ppermute(new, SEQ_AXIS, onward)]
    reduce_scatter x6, waiting for transfers between devices: 76.9 us -> 10.7 us  [scatter(): lax.psum_scatter(grad, SEQ_AXIS, scatter_dimension=0, axis_index_groups=r...]
    dynamic_update_slice x0 -> x54, local copies, waits for them, and re-layouts: none -> 48.5 us  [the longest x30 25.2 us: spread(): lax.dynamic_update_slice_in_dim(whole, twin, (base + 1 - core) * rows_eac...]
    ppermute x0 -> x57, starting transfers between devices: none -> 41.7 us  [the longest x6 18.5 us: spread(): far_high = lax.ppermute(above[:, half:], SEQ_AXIS, backward)]
    pallas_call x2 -> x0, Pallas kernels: 28.3 us -> none  [emit(): pl.pallas_call(emit_kernel, grid=(layers, height // max(height // 4, 8)),...]
    unnamed x308 -> x400, local copies, waits for them, and re-layouts: 40.2 us -> 61.2 us
    all_to_all x12, waiting for transfers between devices: 139 us -> 160 us  [exchange(): return lax.all_to_all(tensor, SEQ_AXIS, 0, 0, tiled=True)]
  transfers between devices with their start and end apart: 25 -> 79, of which waited for: 18 -> 28; matrix products, arithmetic and copies ran while one was open for 26% -> 32% of each run, Pallas kernels for 13% -> 12%
where the time goes in v2:
time: 1180 us; the launch traced here: 1170 us
  waiting for transfers between devices  400 us (34%)
  matrix products  268 us (23%)
  local copies, waits for them, and re-layouts  195 us (17%)
  Pallas kernels  135 us (11%)
  starting transfers between devices  97.5 us (8%)
  other arithmetic  38.2 us (3%)
  blocking collectives  18.3 us (2%)
  between operations  18.2 us (2%)
    dot_general x49, matrix products, contract(): return jnp.einsum(form, left, right, preferred_element_type=F32)  268 us
    all_to_all x12, waiting for transfers between devices, exchange(): return lax.all_to_all(tensor, SEQ_AXIS, 0, 0, tiled=True)  160 us
    all_gather x4, waiting for transfers between devices, body(): n_all = lax.all_gather(norms[c][0].reshape(part, rows, d_model), SEQ_AXIS)  90.4 us
    ppermute x6, waiting for transfers between devices, spread(): below = lax.ppermute(new, SEQ_AXIS, onward)  74.4 us
    pallas_call x4, Pallas kernels, attn_forward(): pl.pallas_call(functools.partial(attn_fwd_kernel, head_dim, blk), grid=(b...  72.1 us
    pallas_call x4, Pallas kernels, attn_backward(): pl.pallas_call(functools.partial(attn_bwd_kernel, head_dim, blk), grid=(b...  62.6 us
    unnamed x400, local copies, waits for them, and re-layouts  61.2 us
    all_to_all x12, starting transfers between devices, exchange(): return lax.all_to_all(tensor, SEQ_AXIS, 0, 0, tiled=True)  54.2 us
  transfers between devices with their start and end apart: 79, of which 28 were waited for; matrix products, arithmetic and copies ran while one was open for 32% of the time, Pallas kernels for 12%

profile of v2, /device:TPU:112, one launch (start us, length us, event | category | flops | bytes accessed | tf_op | source)
XLA Modules:
  0.0 1170.2 jit_solution(3111149025406138593)
XLA Ops:
  14.3 18.3 %all-gather.2 = s32[8,1,128]{2,1,0:T(1,128)S(1)} all-gather(s32[1,1,128]{2,1,0:T(1,128)S(1)} %bitcast.488), channel_id=1, replica_groups=mesh['dp'=2,'sp'=8] {'sp'}, dimensions={0}, use_global_device_ids=true | all-gather | bytes 4608 | tf_op jit(solution)/shard_map/all_gather | solution.py:227
  42.5 10.7 all-gather.12.cloned.1.call-done
  53.2 18.0 %attn_fwd.4 = (bf16[8,3,128,128]{3,2,1,0:T(8,128)(2,1)S(1)}, bf16[8,3,128,128]{3,2,1,0:T(8,128)(2,1)S(1)}, bf16[8,3,128,128]{3,2,1,0:T(8,128)(2,1)S(1)}, bf16[8,...) custom-call(bf16[8,3,128,1024]{3,2,1,0:T(8,128)(2,1)} %bitcast.401, bf16[384,1024]{1,0:T(8,128)(2,1)} %get-tuple-element.197.w_ref, ...), custom_call_target="tpu_custom_call" | custom-call | flops 16106127360 | bytes 6291456 | tf_op jit(solution)/shard_map/attn_fwd/pallas_call | solution.py:114
  74.0 4.7 all-to-all-start
  78.7 20.8 %all-gather.14.cloned.1.call-done = bf16[24,128,1024]{2,1,0:T(8,128)(2,1)} async-done(((bf16[3,128,1024]{2,1,0:T(8,128)(2,1)}), bf16[24,128,1024]{2,1,0:T(8,128)(2,1)}) %all-gather.14.cloned.1.call-update) | async-done | bytes 6291472 | tf_op jit(solution)/shard_map/all_gather | solution.py:282
  99.5 18.0 %attn_fwd.5 = (bf16[8,3,128,128]{3,2,1,0:T(8,128)(2,1)S(1)}, bf16[8,3,128,128]{3,2,1,0:T(8,128)(2,1)S(1)}, bf16[8,3,128,128]{3,2,1,0:T(8,128)(2,1)S(1)}, bf16[8,...) custom-call(bf16[8,3,128,1024]{3,2,1,0:T(8,128)(2,1)} %bitcast.403, bf16[384,1024]{1,0:T(8,128)(2,1)} %get-tuple-element.197.w_ref, ...), custom_call_target="tpu_custom_call" | custom-call | flops 16106127360 | bytes 6291456 | tf_op jit(solution)/shard_map/attn_fwd/pallas_call | solution.py:114
  126.8 10.9 fusion.67
  148.1 19.9 %fusion.83 = (bf16[384,4096]{1,0:T(8,128)(2,1)S(1)}, f32[384,4096]{1,0:T(8,128)}) fusion(bf16[384,1024]{1,0:T(8,128)(2,1)S(1)} %fusion.170, bf16[2,1024,4096]{2,1,0:T(8,128)(2,1)} %param.19), kind=kOutput, calls=%fused_computation.109 | convolution fusion | flops 3235381248 | bytes 18612224 | tf_op jit(solution)/shard_map/td,df->tf/dot_general | solution.py:23
  174.4 37.7 %all-gather.10.cloned.1.call-done.n_ref = bf16[8,3,128,1024]{3,2,1,0:T(8,128)(2,1)} async-done(((bf16[1,3,128,1024]{3,2,1,0:T(8,128)(2,1)}), bf16[8,3,128,1024]{3,2,1,0:T(8,128)(2,1)}) %all-gather.10.cloned.1.call-update) | async-done | bytes 6291472 | tf_op jit(solution)/shard_map/all_gather | solution.py:282
  212.2 18.0 %attn_fwd.7 = (bf16[8,3,128,128]{3,2,1,0:T(8,128)(2,1)S(1)}, bf16[8,3,128,128]{3,2,1,0:T(8,128)(2,1)S(1)}, bf16[8,3,128,128]{3,2,1,0:T(8,128)(2,1)S(1)}, bf16[8,...) custom-call(bf16[8,3,128,1024]{3,2,1,0:T(8,128)(2,1)} %all-gather.10.cloned.1.call-done.n_ref, ...), custom_call_target="tpu_custom_call" | custom-call | flops 16106127360 | bytes 6291456 | tf_op jit(solution)/shard_map/attn_fwd/pallas_call | solution.py:114
  237.4 21.1 %all-gather.8.cloned.1.call-done.n_ref = bf16[8,3,128,1024]{3,2,1,0:T(8,128)(2,1)} async-done(((bf16[1,3,128,1024]{3,2,1,0:T(8,128)(2,1)}), bf16[8,3,128,1024]{3,2,1,0:T(8,128)(2,1)}) %all-gather.8.cloned.1.call-update) | async-done | bytes 6291472 | tf_op jit(solution)/shard_map/all_gather | solution.py:282
  258.5 18.0 %attn_fwd.6 = (bf16[8,3,128,128]{3,2,1,0:T(8,128)(2,1)S(1)}, bf16[8,3,128,128]{3,2,1,0:T(8,128)(2,1)S(1)}, bf16[8,3,128,128]{3,2,1,0:T(8,128)(2,1)S(1)}, bf16[8,...) custom-call(bf16[8,3,128,1024]{3,2,1,0:T(8,128)(2,1)} %all-gather.8.cloned.1.call-done.n_ref, ...), custom_call_target="tpu_custom_call" | custom-call | flops 16106127360 | bytes 6291456 | tf_op jit(solution)/shard_map/attn_fwd/pallas_call | solution.py:114
  286.1 10.4 all-to-all-done.2
  304.7 12.3 %fusion.91 = (bf16[384,4096]{1,0:T(8,128)(2,1)}, f32[384,4096]{1,0:T(8,128)}) fusion(bf16[384,1024]{1,0:T(8,128)(2,1)S(1)} %get-tuple-element.208, bf16[2,1024,4096]{2,1,0:T(8,128)(2,1)} %param.19), kind=kOutput, calls=%fused_computation.117 | convolution fusion | flops 3235381248 | bytes 18612224 | tf_op jit(solution)/shard_map/td,df->tf/dot_general | solution.py:23
  317.0 6.4 fusion.75
  325.1 12.3 %fusion.94 = f32[4096,1024]{1,0:T(8,128)} fusion(bf16[768,1024]{1,0:T(8,128)(2,1)S(1)} %bitcast.460, bf16[384,4096]{1,0:T(8,128)(2,1)} %get-tuple-element.239, bf16[384,4096]{1,0:T(8,128)(2,1)S(1)} %get-tuple-element.241), kind=kOutput, calls=%fused_computation.121 | convolution fusion | flops 6455033856 | bytes 24641536 | tf_op jit(solution)/shard_map/tf,td->fd/dot_general | solution.py:23
  339.6 11.3 fusion.38
  351.0 10.3 fusion.45
  363.0 10.6 fusion.98
  373.7 8.3 fusion.167
  390.3 8.3 fusion.194
  402.2 5.6 all-to-all-done.4.d_ref
  407.8 4.6 all-to-all-start.5
  412.4 5.2 fusion.314
  424.2 5.7 all-to-all-done.5.d_ref
  433.4 15.6 %attn_bwd.4 = bf16[8,3,3,128,128]{4,3,2,1,0:T(8,128)(2,1)} custom-call(bf16[8,3,128,128]{3,2,1,0:T(8,128)(2,1)S(1)} %copy-done.13, bf16[8,3,128,128]{3,2,1,0:T(8,128)(2,1)S(1)} %copy-done.15, bf16[8,3,128,128]{3,2,1,0:T(8,128)(2,1)S(1)} %copy-done.17, bf16[8,3,128,128]{3,2,1,0:T(8,128)(2,1)} %get-tuple-element.69.o_ref, ...), custom_call_target="tpu_custom_call" | custom-call | flops 16106127360 | bytes 6291456 | tf_op jit(solution)/shard_map/attn_bwd/pallas_call | solution.py:190
  449.1 4.5 all-to-all-start.6
  453.6 5.1 fusion.315
  458.7 4.6 fusion.266
  463.6 15.6 %attn_bwd.5 = bf16[8,3,3,128,128]{4,3,2,1,0:T(8,128)(2,1)} custom-call(bf16[8,3,128,128]{3,2,1,0:T(8,128)(2,1)S(1)} %copy-done.7, bf16[8,3,128,128]{3,2,1,0:T(8,128)(2,1)S(1)} %copy-done.9, bf16[8,3,128,128]{3,2,1,0:T(8,128)(2,1)S(1)} %copy-done.11, bf16[8,3,128,128]{3,2,1,0:T(8,128)(2,1)} %get-tuple-element.71.o_ref, ...), custom_call_target="tpu_custom_call" | custom-call | flops 16106127360 | bytes 6291456 | tf_op jit(solution)/shard_map/attn_bwd/pallas_call | solution.py:190
  479.3 17.2 %all-to-all-done.6 = bf16[8,3,3,128,128]{4,3,2,1,0:T(8,128)(2,1)} async-done(((bf16[8,3,3,128,128]{4,3,2,1,0:T(8,128)(2,1)}), bf16[8,3,3,128,128]{4,3,2,1,0:T(8,128)(2,1)}, u32[]{:S(2)}, u32[]{:S(2)}) %all-to-all-start.6) | async-done | bytes 2359328 | tf_op jit(solution)/shard_map/all_to_all | solution.py:208
  496.4 4.6 all-to-all-start.7
  501.1 6.3 fusion.102
  507.4 6.6 bitcast_add_fusion.1
  514.0 29.8 %all-to-all-done.7 = bf16[8,3,3,128,128]{4,3,2,1,0:T(8,128)(2,1)} async-done(((bf16[8,3,3,128,128]{4,3,2,1,0:T(8,128)(2,1)}), bf16[8,3,3,128,128]{4,3,2,1,0:T(8,128)(2,1)}, u32[]{:S(2)}, u32[]{:S(2)}) %all-to-all-start.7) | async-done | bytes 2359328 | tf_op jit(solution)/shard_map/all_to_all | solution.py:208
  579.0 8.6 fusion.129
  587.7 11.5 fusion.52
  599.3 11.4 fusion.59
  610.7 11.3 convolution_add_fusion.1
  630.3 6.0 fusion.275
  641.0 6.1 fusion.149
  655.2 8.4 fusion.176
  669.7 7.3 all-to-all-done.8.d_ref
  681.9 13.0 %convolution_add_fusion = f32[512,4096]{1,0:T(8,128)} fusion(f32[512,4096]{1,0:T(8,128)} %collective-permute-done.1, bf16[768,4096]{1,0:T(8,128)(2,1)} %copy-done.36, pred[]{:T(512)S(6)} %eq.43, bf16[768,128]{1,0:T(8,128)(2,1)} %copy-done.130, bf16[768,128]{1,0:T(8,128)(2,1)} %copy-done.129, bf16[768,128]{1,0:T(8,128)(2,1)} %copy-done.128, ...), kind=kOutput, calls=%fused_computation.133 | convolution fusion | flops 3231973376 | bytes 26017792 | tf_op jit(solution)/shard_map/tf,td->fd/dot_general | solution.py:23
  694.9 8.3 all-to-all-done.9.d_ref
  706.7 15.6 %attn_bwd.6 = bf16[8,3,3,128,128]{4,3,2,1,0:T(8,128)(2,1)} custom-call(bf16[8,3,128,128]{3,2,1,0:T(8,128)(2,1)S(1)} %copy-done.1, bf16[8,3,128,128]{3,2,1,0:T(8,128)(2,1)S(1)} %copy-done.3, bf16[8,3,128,128]{3,2,1,0:T(8,128)(2,1)S(1)} %copy-done.5, bf16[8,3,128,128]{3,2,1,0:T(8,128)(2,1)} %get-tuple-element.66.o_ref, ...), custom_call_target="tpu_custom_call" | custom-call | flops 16106127360 | bytes 6291456 | tf_op jit(solution)/shard_map/attn_bwd/pallas_call | solution.py:190
  722.4 4.9 all-to-all-start.10
  730.9 15.6 %attn_bwd.7 = bf16[8,3,3,128,128]{4,3,2,1,0:T(8,128)(2,1)} custom-call(bf16[8,3,128,128]{3,2,1,0:T(8,128)(2,1)S(1)} %get-tuple-element.105.q_ref, bf16[8,3,128,128]{3,2,1,0:T(8,128)(2,1)S(1)} %get-tuple-element.106.k_ref, bf16[8,3,128,128]{3,2,1,0:T(8,128)(2,1)S(1)} %get-tuple-element.107.v_ref, bf16[8,3,128,128]{3,2,1,0:T(8,128)(2,1)} %get-tuple-element.67.o_ref, ...), custom_call_target="tpu_custom_call" | custom-call | flops 16106127360 | bytes 6291456 | tf_op jit(solution)/shard_map/attn_bwd/pallas_call | solution.py:190
  746.5 36.3 %all-to-all-done.10 = bf16[8,3,3,128,128]{4,3,2,1,0:T(8,128)(2,1)} async-done(((bf16[8,3,3,128,128]{4,3,2,1,0:T(8,128)(2,1)}), bf16[8,3,3,128,128]{4,3,2,1,0:T(8,128)(2,1)}, u32[]{:S(2)}, u32[]{:S(2)}) %all-to-all-start.10) | async-done | bytes 2359328 | tf_op jit(solution)/shard_map/all_to_all | solution.py:208
  782.9 4.5 all-to-all-start.11
  790.3 4.9 fusion.333
  795.2 5.0 bitcast_add_fusion
  803.7 39.3 %all-to-all-done.11 = bf16[8,3,3,128,128]{4,3,2,1,0:T(8,128)(2,1)} async-done(((bf16[8,3,3,128,128]{4,3,2,1,0:T(8,128)(2,1)}), bf16[8,3,3,128,128]{4,3,2,1,0:T(8,128)(2,1)}, u32[]{:S(2)}, u32[]{:S(2)}) %all-to-all-start.11) | async-done | bytes 2359328 | tf_op jit(solution)/shard_map/all_to_all | solution.py:208
  882.3 8.2 reduce-scatter.17.cloned.1.call-done
  909.8 4.5 collective-permute-done.15
  916.5 9.1 collective-permute-done.24
  928.8 8.0 collective-permute-done.33
  937.1 7.7 fusion.189
  970.1 5.6 copy-done.30
  1014.4 27.0 %collective-permute-done.40 = bf16[2,128,4096]{2,1,0:T(8,128)(2,1)S(1)} collective-permute-done((bf16[2,128,4096]{2,1,0:T(8,128)(2,1)S(1)}, bf16[2,128,4096]{2,1,0:T(8,128)(2,1)S(1)}, u32[]{:S(2)}, u32[]{:S(2)}) %collective-permute-start.40) | collective-permute-done | bytes 2097184 | tf_op jit(solution)/shard_map/ppermute | solution.py:375
  1041.4 44.4 %collective-permute-done.49 = bf16[2,512,1024]{2,1,0:T(8,128)(2,1)S(1)} collective-permute-done((bf16[2,512,1024]{2,1,0:T(8,128)(2,1)S(1)}, bf16[2,512,1024]{2,1,0:T(8,128)(2,1)S(1)}, u32[]{:S(2)}, u32[]{:S(2)}) %collective-permute-start.49) | collective-permute-done | bytes 2097184 | tf_op jit(solution)/shard_map/ppermute | solution.py:375
  1101.8 17.7 %collective-permute-done.44 = bf16[2,64,4096]{2,1,0:T(8,128)(2,1)S(1)} collective-permute-done((bf16[2,64,4096]{2,1,0:T(8,128)(2,1)S(1)}, bf16[2,64,4096]{2,1,0:T(8,128)(2,1)S(1)}, u32[]{:S(2)}, u32[]{:S(2)}) %collective-permute-start.44) | collective-permute-done | bytes 1048608 | tf_op jit(solution)/shard_map/ppermute | solution.py:377
  1125.7 19.3 %collective-permute-done.53 = bf16[2,256,1024]{2,1,0:T(8,128)(2,1)S(1)} collective-permute-done((bf16[2,256,1024]{2,1,0:T(8,128)(2,1)S(1)}, bf16[2,256,1024]{2,1,0:T(8,128)(2,1)S(1)}, u32[]{:S(2)}, u32[]{:S(2)}) %collective-permute-start.53) | collective-permute-done | bytes 1048608 | tf_op jit(solution)/shard_map/ppermute | solution.py:377
  1156.7 6.2 copy-done.29
  (729 shorter events, 338.8 us)
Async XLA Ops:
  7.2 46.1 %all-gather.12.cloned.1.call-start = ((), (), s32[]{:S(2)}) async-start(), calls=%async_computation.26 | async-start | bytes 7077888 | tf_op jit(solution)/shard_map/all_gather | solution.py:282
  13.4 86.1 %all-gather.14.cloned.1.call-start = ((), (), s32[]{:S(2)}) async-start(), calls=%async_computation.27 | async-start | bytes 7077888 | tf_op jit(solution)/shard_map/all_gather | solution.py:282
  74.0 43.5 %all-to-all-start = ((bf16[8,3,128,128]{3,2,1,0:T(8,128)(2,1)}), bf16[8,3,128,128]{3,2,1,0:T(8,128)(2,1)}, u32[]{:S(2)}, u32[]{:S(2)}) async-start(bf16[8,3,128,128]{3,2,1,0:T(8,128)(2,1)} %get-tuple-element.66.o_ref), calls=%async_computation | async-start | bytes 1572864 | tf_op jit(solution)/shard_map/all_to_all | solution.py:208
  117.5 25.8 %all-to-all-start.1 = ((bf16[8,3,128,128]{3,2,1,0:T(8,128)(2,1)}), bf16[8,3,128,128]{3,2,1,0:T(8,128)(2,1)}, u32[]{:S(2)}, u32[]{:S(2)}) async-start(bf16[8,3,128,128]{3,2,1,0:T(8,128)(2,1)} %get-tuple-element.67.o_ref), calls=%async_computation.1 | async-start | bytes 1572864 | tf_op jit(solution)/shard_map/all_to_all | solution.py:208
  122.0 90.2 %all-gather.10.cloned.1.call-start = ((), (), s32[]{:S(2)}) async-start(), calls=%async_computation.19 | async-start | bytes 7077888 | tf_op jit(solution)/shard_map/all_gather | solution.py:282
  173.8 84.6 %all-gather.8.cloned.1.call-start = ((), (), s32[]{:S(2)}) async-start(), calls=%async_computation.18 | async-start | bytes 7077888 | tf_op jit(solution)/shard_map/all_gather | solution.py:282
  232.9 46.2 %all-to-all-start.3 = ((bf16[8,3,128,128]{3,2,1,0:T(8,128)(2,1)}), bf16[8,3,128,128]{3,2,1,0:T(8,128)(2,1)}, u32[]{:S(2)}, u32[]{:S(2)}) async-start(bf16[8,3,128,128]{3,2,1,0:T(8,128)(2,1)} %get-tuple-element.71.o_ref), calls=%async_computation.3 | async-start | bytes 1572864 | tf_op jit(solution)/shard_map/all_to_all | solution.py:208
  279.1 17.4 %all-to-all-start.2 = ((bf16[8,3,128,128]{3,2,1,0:T(8,128)(2,1)}), bf16[8,3,128,128]{3,2,1,0:T(8,128)(2,1)}, u32[]{:S(2)}, u32[]{:S(2)}) async-start(bf16[8,3,128,128]{3,2,1,0:T(8,128)(2,1)} %get-tuple-element.69.o_ref), calls=%async_computation.2 | async-start | bytes 1572864 | tf_op jit(solution)/shard_map/all_to_all | solution.py:208
  283.5 260.3 %reduce-scatter.7.cloned.1.call-start = ((), (), s32[]{:S(2)}) async-start(), calls=%async_computation.20 | async-start | bytes 18874368 | tf_op jit(solution)/shard_map/reduce_scatter | solution.py:274
  337.4 299.0 %reduce-scatter.9.cloned.1.call-start = ((), (), s32[]{:S(2)}) async-start(), calls=%async_computation.21 | async-start | bytes 18874368 | tf_op jit(solution)/shard_map/reduce_scatter | solution.py:274
  385.8 21.9 %all-to-all-start.4 = ((bf16[8,3,128,128]{3,2,1,0:T(8,128)(2,1)}), bf16[8,3,128,128]{3,2,1,0:T(8,128)(2,1)}, u32[]{:S(2)}, u32[]{:S(2)}) async-start(bf16[8,3,128,128]{3,2,1,0:T(8,128)(2,1)} %bitcast.433), calls=%async_computation.4 | async-start | bytes 1572864 | tf_op jit(solution)/shard_map/all_to_all | solution.py:208
  407.8 22.2 %all-to-all-start.5 = ((bf16[8,3,128,128]{3,2,1,0:T(8,128)(2,1)}), bf16[8,3,128,128]{3,2,1,0:T(8,128)(2,1)}, u32[]{:S(2)}, u32[]{:S(2)}) async-start(bf16[8,3,128,128]{3,2,1,0:T(8,128)(2,1)} %bitcast.434), calls=%async_computation.5 | async-start | bytes 1572864 | tf_op jit(solution)/shard_map/all_to_all | solution.py:208
  449.1 47.4 %all-to-all-start.6 = ((bf16[8,3,3,128,128]{4,3,2,1,0:T(8,128)(2,1)}), bf16[8,3,3,128,128]{4,3,2,1,0:T(8,128)(2,1)}, u32[]{:S(2)}, u32[]{:S(2)}) async-start(bf16[8,3,3,128,128]{4,3,2,1,0:T(8,128)(2,1)} %attn_bwd.4), calls=%async_computation.6 | async-start | bytes 4718592 | tf_op jit(solution)/shard_map/all_to_all | solution.py:208
  496.4 47.4 %all-to-all-start.7 = ((bf16[8,3,3,128,128]{4,3,2,1,0:T(8,128)(2,1)}), bf16[8,3,3,128,128]{4,3,2,1,0:T(8,128)(2,1)}, u32[]{:S(2)}, u32[]{:S(2)}) async-start(bf16[8,3,3,128,128]{4,3,2,1,0:T(8,128)(2,1)} %attn_bwd.5), calls=%async_computation.7 | async-start | bytes 4718592 | tf_op jit(solution)/shard_map/all_to_all | solution.py:208
  501.0 194.0 %reduce-scatter.11.cloned.1.call-start = ((), (), s32[]{:S(2)}) async-start(), calls=%async_computation.22 | async-start | bytes 4718592 | tf_op jit(solution)/shard_map/reduce_scatter | solution.py:274
  587.6 23.1 %collective-permute-start = (f32[2048,1024]{1,0:T(8,128)}, f32[2048,1024]{1,0:T(8,128)}, u32[]{:S(2)}, u32[]{:S(2)}) collective-permute-start(f32[2048,1024]{1,0:T(8,128)} %fusion.129), channel_id=1, source_target_pairs={{0,1},{1,0},{2,3},{3,2},{4,5},{5,4},{6,7},{7,6},{8,9},{9,8},{10,11... | collective-permute-start | bytes 25165832 | tf_op jit(solution)/shard_map/ppermute | solution.py:271
  587.7 255.3 %reduce-scatter.13.cloned.1.call-start = ((), (), s32[]{:S(2)}) async-start(), calls=%async_computation.23 | async-start | bytes 10485760 | tf_op jit(solution)/shard_map/reduce_scatter | solution.py:274
  636.4 45.5 %collective-permute-start.1 = (f32[512,4096]{1,0:T(8,128)}, f32[512,4096]{1,0:T(8,128)}, u32[]{:S(2)}, u32[]{:S(2)}) collective-permute-start(f32[512,4096]{1,0:T(8,128)} %fusion.275), channel_id=1, source_target_pairs={{0,1},{1,0},{2,3},{3,2},{4,5},{5,4},{6,7},{7,6},{8,9},{9,8},{10,11... | collective-permute-start | bytes 25165832 | tf_op jit(solution)/shard_map/ppermute | solution.py:271
  650.8 26.2 %all-to-all-start.8 = ((bf16[8,3,128,128]{3,2,1,0:T(8,128)(2,1)}), bf16[8,3,128,128]{3,2,1,0:T(8,128)(2,1)}, u32[]{:S(2)}, u32[]{:S(2)}) async-start(bf16[8,3,128,128]{3,2,1,0:T(8,128)(2,1)} %bitcast.432), calls=%async_computation.10 | async-start | bytes 1572864 | tf_op jit(solution)/shard_map/all_to_all | solution.py:208
  677.0 26.2 %all-to-all-start.9 = ((bf16[8,3,128,128]{3,2,1,0:T(8,128)(2,1)}), bf16[8,3,128,128]{3,2,1,0:T(8,128)(2,1)}, u32[]{:S(2)}, u32[]{:S(2)}) async-start(bf16[8,3,128,128]{3,2,1,0:T(8,128)(2,1)} %bitcast.431), calls=%async_computation.11 | async-start | bytes 1572864 | tf_op jit(solution)/shard_map/all_to_all | solution.py:208
  681.4 164.0 %reduce-scatter.15.cloned.1.call-start = ((), (), s32[]{:S(2)}) async-start(), calls=%async_computation.24 | async-start | bytes 10485760 | tf_op jit(solution)/shard_map/reduce_scatter | solution.py:274
  722.4 60.5 %all-to-all-start.10 = ((bf16[8,3,3,128,128]{4,3,2,1,0:T(8,128)(2,1)}), bf16[8,3,3,128,128]{4,3,2,1,0:T(8,128)(2,1)}, u32[]{:S(2)}, u32[]{:S(2)}) async-start(bf16[8,3,3,128,128]{4,3,2,1,0:T(8,128)(2,1)} %attn_bwd.6), calls=%async_computation.13 | async-start | bytes 4718592 | tf_op jit(solution)/shard_map/all_to_all | solution.py:208
  730.5 69.7 %collective-permute-start.2 = (f32[512,1024]{1,0:T(8,128)}, f32[512,1024]{1,0:T(8,128)}, u32[]{:S(2)}, u32[]{:S(2)}) collective-permute-start(f32[512,1024]{1,0:T(8,128)} %fusion.260), channel_id=1, source_target_pairs={{0,1},{1,0},{2,3},{3,2},{4,5},{5,4},{6,7},{7,6},{8,9},{9,8},{10,11... | collective-permute-start | bytes 6291464 | tf_op jit(solution)/shard_map/ppermute | solution.py:271
  782.9 60.1 %all-to-all-start.11 = ((bf16[8,3,3,128,128]{4,3,2,1,0:T(8,128)(2,1)}), bf16[8,3,3,128,128]{4,3,2,1,0:T(8,128)(2,1)}, u32[]{:S(2)}, u32[]{:S(2)}) async-start(bf16[8,3,3,128,128]{4,3,2,1,0:T(8,128)(2,1)} %attn_bwd.7), calls=%async_computation.14 | async-start | bytes 4718592 | tf_op jit(solution)/shard_map/all_to_all | solution.py:208
  787.4 103.0 %reduce-scatter.17.cloned.1.call-start = ((), (), s32[]{:S(2)}) async-start(), calls=%async_computation.25 | async-start | bytes 2621440 | tf_op jit(solution)/shard_map/reduce_scatter | solution.py:274
  849.1 50.2 %collective-permute-start.3 = (bf16[2,128,1024]{2,1,0:T(8,128)(2,1)}, bf16[2,128,1024]{2,1,0:T(8,128)(2,1)}, u32[]{:S(2)}, u32[]{:S(2)}) collective-permute-start(bf16[2,128,1024]{2,1,0:T(8,128)(2,1)} %get-tuple-element.141), channel_id=1, source_target_pairs={{0,1},{1,0},{2,3},{3,2},{4,5},{5,4},{6,7},{7,6},{8,9},{9,8},{10,11... | collective-permute-start | bytes 1572872 | tf_op jit(solution)/shard_map/ppermute | solution.py:381
  849.1 51.0 %collective-permute-start.4 = (bf16[2,128,1024]{2,1,0:T(8,128)(2,1)}, bf16[2,128,1024]{2,1,0:T(8,128)(2,1)}, u32[]{:S(2)}, u32[]{:S(2)}) collective-permute-start(bf16[2,128,1024]{2,1,0:T(8,128)(2,1)} %get-tuple-element.141), channel_id=1, source_target_pairs={{0,2},{1,3},{2,4},{3,5},{4,6},{5,7},{6,0},{7,1},{8,10},{9,11},{10,... | collective-permute-start | bytes 1572872 | tf_op jit(solution)/shard_map/ppermute | solution.py:375
  849.4 52.0 %collective-permute-start.6 = (bf16[2,128,1024]{2,1,0:T(8,128)(2,1)}, bf16[2,128,1024]{2,1,0:T(8,128)(2,1)}, u32[]{:S(2)}, u32[]{:S(2)}) collective-permute-start(bf16[2,128,1024]{2,1,0:T(8,128)(2,1)} %get-tuple-element.141), channel_id=1, source_target_pairs={{0,6},{1,7},{2,0},{3,1},{4,2},{5,3},{6,4},{7,5},{8,14},{9,15},{10,... | collective-permute-start | bytes 1572872 | tf_op jit(solution)/shard_map/ppermute | solution.py:376
  855.9 47.5 %collective-permute-start.12 = (bf16[2,128,1024]{2,1,0:T(8,128)(2,1)}, bf16[2,128,1024]{2,1,0:T(8,128)(2,1)}, u32[]{:S(2)}, u32[]{:S(2)}) collective-permute-start(bf16[2,128,1024]{2,1,0:T(8,128)(2,1)} %get-tuple-element.139), channel_id=1, source_target_pairs={{0,1},{1,0},{2,3},{3,2},{4,5},{5,4},{6,7},{7,6},{8,9},{9,8},{10,11... | collective-permute-start | bytes 1572872 | tf_op jit(solution)/shard_map/ppermute | solution.py:381
  856.0 47.5 %collective-permute-start.13 = (bf16[2,128,1024]{2,1,0:T(8,128)(2,1)}, bf16[2,128,1024]{2,1,0:T(8,128)(2,1)}, u32[]{:S(2)}, u32[]{:S(2)}) collective-permute-start(bf16[2,128,1024]{2,1,0:T(8,128)(2,1)} %get-tuple-element.139), channel_id=1, source_target_pairs={{0,2},{1,3},{2,4},{3,5},{4,6},{5,7},{6,0},{7,1},{8,10},{9,11},{10,... | collective-permute-start | bytes 1572872 | tf_op jit(solution)/shard_map/ppermute | solution.py:375
  899.3 15.0 %collective-permute-start.15 = (bf16[2,128,1024]{2,1,0:T(8,128)(2,1)}, bf16[2,128,1024]{2,1,0:T(8,128)(2,1)S(1)}, u32[]{:S(2)}, u32[]{:S(2)}) collective-permute-start(bf16[2,128,1024]{2,1,0:T(8,128)(2,1)} %get-tuple-element.139), channel_id=1, source_target_pairs={{0,6},{1,7},{2,0},{3,1},{4,2},{5,3},{6,4},{7,5},{8,14},{9,15},{10,... | collective-permute-start | bytes 1572872 | tf_op jit(solution)/shard_map/ppermute | solution.py:376
  900.2 16.3 %collective-permute-start.22 = (bf16[2,128,1024]{2,1,0:T(8,128)(2,1)}, bf16[2,128,1024]{2,1,0:T(8,128)(2,1)}, u32[]{:S(2)}, u32[]{:S(2)}) collective-permute-start(bf16[2,128,1024]{2,1,0:T(8,128)(2,1)} %get-tuple-element.137), channel_id=1, source_target_pairs={{0,2},{1,3},{2,4},{3,5},{4,6},{5,7},{6,0},{7,1},{8,10},{9,11},{10,... | collective-permute-start | bytes 1572872 | tf_op jit(solution)/shard_map/ppermute | solution.py:375
  901.3 24.2 %collective-permute-start.24 = (bf16[2,128,1024]{2,1,0:T(8,128)(2,1)}, bf16[2,128,1024]{2,1,0:T(8,128)(2,1)S(1)}, u32[]{:S(2)}, u32[]{:S(2)}) collective-permute-start(bf16[2,128,1024]{2,1,0:T(8,128)(2,1)} %get-tuple-element.137), channel_id=1, source_target_pairs={{0,6},{1,7},{2,0},{3,1},{4,2},{5,3},{6,4},{7,5},{8,14},{9,15},{10,... | collective-permute-start | bytes 1572872 | tf_op jit(solution)/shard_map/ppermute | solution.py:376
  903.4 23.0 %collective-permute-start.31 = (bf16[2,128,1024]{2,1,0:T(8,128)(2,1)}, bf16[2,128,1024]{2,1,0:T(8,128)(2,1)}, u32[]{:S(2)}, u32[]{:S(2)}) collective-permute-start(bf16[2,128,1024]{2,1,0:T(8,128)(2,1)} %get-tuple-element.135), channel_id=1, source_target_pairs={{0,2},{1,3},{2,4},{3,5},{4,6},{5,7},{6,0},{7,1},{8,10},{9,11},{10,... | collective-permute-start | bytes 1572872 | tf_op jit(solution)/shard_map/ppermute | solution.py:375
  903.4 33.4 %collective-permute-start.33 = (bf16[2,128,1024]{2,1,0:T(8,128)(2,1)}, bf16[2,128,1024]{2,1,0:T(8,128)(2,1)S(1)}, u32[]{:S(2)}, u32[]{:S(2)}) collective-permute-start(bf16[2,128,1024]{2,1,0:T(8,128)(2,1)} %get-tuple-element.135), channel_id=1, source_target_pairs={{0,6},{1,7},{2,0},{3,1},{4,2},{5,3},{6,4},{7,5},{8,14},{9,15},{10,... | collective-permute-start | bytes 1572872 | tf_op jit(solution)/shard_map/ppermute | solution.py:376
  914.3 32.6 %collective-permute-start.21 = (bf16[2,128,1024]{2,1,0:T(8,128)(2,1)}, bf16[2,128,1024]{2,1,0:T(8,128)(2,1)S(1)}, u32[]{:S(2)}, u32[]{:S(2)}) collective-permute-start(bf16[2,128,1024]{2,1,0:T(8,128)(2,1)} %get-tuple-element.137), channel_id=1, source_target_pairs={{0,1},{1,0},{2,3},{3,2},{4,5},{5,4},{6,7},{7,6},{8,9},{9,8},{10,11... | collective-permute-start | bytes 1572872 | tf_op jit(solution)/shard_map/ppermute | solution.py:381
  916.5 33.7 %collective-permute-start.30 = (bf16[2,128,1024]{2,1,0:T(8,128)(2,1)}, bf16[2,128,1024]{2,1,0:T(8,128)(2,1)S(1)}, u32[]{:S(2)}, u32[]{:S(2)}) collective-permute-start(bf16[2,128,1024]{2,1,0:T(8,128)(2,1)} %get-tuple-element.135), channel_id=1, source_target_pairs={{0,1},{1,0},{2,3},{3,2},{4,5},{5,4},{6,7},{7,6},{8,9},{9,8},{10,11... | collective-permute-start | bytes 1572872 | tf_op jit(solution)/shard_map/ppermute | solution.py:381
  925.5 24.6 %collective-permute-start.8 = (bf16[2,64,1024]{2,1,0:T(8,128)(2,1)S(1)}, bf16[2,64,1024]{2,1,0:T(8,128)(2,1)S(1)}, u32[]{:S(2)}, u32[]{:S(2)}) collective-permute-start(bf16[2,64,1024]{2,1,0:T(8,128)(2,1)S(1)} %slice.428), channel_id=1, source_target_pairs={{0,2},{1,3},{2,4},{3,5},{4,6},{5,7},{6,0},{7,1},{8,10},{9,11},{10,... | collective-permute-start | bytes 786440 | tf_op jit(solution)/shard_map/ppermute | solution.py:377
  926.4 27.0 %collective-permute-start.10 = (bf16[2,64,1024]{2,1,0:T(8,128)(2,1)S(1)}, bf16[2,64,1024]{2,1,0:T(8,128)(2,1)S(1)}, u32[]{:S(2)}, u32[]{:S(2)}) collective-permute-start(bf16[2,64,1024]{2,1,0:T(8,128)(2,1)S(1)} %slice.429), channel_id=1, source_target_pairs={{0,6},{1,7},{2,0},{3,1},{4,2},{5,3},{6,4},{7,5},{8,14},{9,15},{10,... | collective-permute-start | bytes 786440 | tf_op jit(solution)/shard_map/ppermute | solution.py:378
  936.8 16.6 %collective-permute-start.17 = (bf16[2,64,1024]{2,1,0:T(8,128)(2,1)S(1)}, bf16[2,64,1024]{2,1,0:T(8,128)(2,1)S(1)}, u32[]{:S(2)}, u32[]{:S(2)}) collective-permute-start(bf16[2,64,1024]{2,1,0:T(8,128)(2,1)S(1)} %slice.430), channel_id=1, source_target_pairs={{0,2},{1,3},{2,4},{3,5},{4,6},{5,7},{6,0},{7,1},{8,10},{9,11},{10,... | collective-permute-start | bytes 786440 | tf_op jit(solution)/shard_map/ppermute | solution.py:377
  946.9 14.5 %collective-permute-start.19 = (bf16[2,64,1024]{2,1,0:T(8,128)(2,1)S(1)}, bf16[2,64,1024]{2,1,0:T(8,128)(2,1)S(1)}, u32[]{:S(2)}, u32[]{:S(2)}) collective-permute-start(bf16[2,64,1024]{2,1,0:T(8,128)(2,1)S(1)} %slice.431), channel_id=1, source_target_pairs={{0,6},{1,7},{2,0},{3,1},{4,2},{5,3},{6,4},{7,5},{8,14},{9,15},{10,... | collective-permute-start | bytes 786440 | tf_op jit(solution)/shard_map/ppermute | solution.py:378
  950.2 11.9 %collective-permute-start.28 = (bf16[2,64,1024]{2,1,0:T(8,128)(2,1)S(1)}, bf16[2,64,1024]{2,1,0:T(8,128)(2,1)S(1)}, u32[]{:S(2)}, u32[]{:S(2)}) collective-permute-start(bf16[2,64,1024]{2,1,0:T(8,128)(2,1)S(1)} %slice.433), channel_id=1, source_target_pairs={{0,6},{1,7},{2,0},{3,1},{4,2},{5,3},{6,4},{7,5},{8,14},{9,15},{10,... | collective-permute-start | bytes 786440 | tf_op jit(solution)/shard_map/ppermute | solution.py:378
  953.4 11.5 collective-permute-start.37
  961.4 19.3 %collective-permute-start.11 = (bf16[2,64,1024]{2,1,0:T(8,128)(2,1)S(1)}, bf16[2,64,1024]{2,1,0:T(8,128)(2,1)S(1)}, u32[]{:S(2)}, u32[]{:S(2)}) collective-permute-start(bf16[2,64,1024]{2,1,0:T(8,128)(2,1)S(1)} %collective-permute-done.10), channel_id=1, source_target_pairs={{0,1},{1,0},{2,3},{3,2},{4,5},{5,4},{6,7},{7,6},{8,9},{9,8},{10,11... | collective-permute-start | bytes 786440 | tf_op jit(solution)/shard_map/ppermute | solution.py:382
  962.1 19.2 %collective-permute-start.18 = (bf16[2,64,1024]{2,1,0:T(8,128)(2,1)S(1)}, bf16[2,64,1024]{2,1,0:T(8,128)(2,1)S(1)}, u32[]{:S(2)}, u32[]{:S(2)}) collective-permute-start(bf16[2,64,1024]{2,1,0:T(8,128)(2,1)S(1)} %collective-permute-done.17), channel_id=1, source_target_pairs={{0,1},{1,0},{2,3},{3,2},{4,5},{5,4},{6,7},{7,6},{8,9},{9,8},{10,11... | collective-permute-start | bytes 786440 | tf_op jit(solution)/shard_map/ppermute | solution.py:382
  962.7 18.7 %collective-permute-start.20 = (bf16[2,64,1024]{2,1,0:T(8,128)(2,1)S(1)}, bf16[2,64,1024]{2,1,0:T(8,128)(2,1)S(1)}, u32[]{:S(2)}, u32[]{:S(2)}) collective-permute-start(bf16[2,64,1024]{2,1,0:T(8,128)(2,1)S(1)} %collective-permute-done.19), channel_id=1, source_target_pairs={{0,1},{1,0},{2,3},{3,2},{4,5},{5,4},{6,7},{7,6},{8,9},{9,8},{10,11... | collective-permute-start | bytes 786440 | tf_op jit(solution)/shard_map/ppermute | solution.py:382
  964.9 17.0 %collective-permute-start.27 = (bf16[2,64,1024]{2,1,0:T(8,128)(2,1)S(1)}, bf16[2,64,1024]{2,1,0:T(8,128)(2,1)S(1)}, u32[]{:S(2)}, u32[]{:S(2)}) collective-permute-start(bf16[2,64,1024]{2,1,0:T(8,128)(2,1)S(1)} %collective-permute-done.26), channel_id=1, source_target_pairs={{0,1},{1,0},{2,3},{3,2},{4,5},{5,4},{6,7},{7,6},{8,9},{9,8},{10,11... | collective-permute-start | bytes 786440 | tf_op jit(solution)/shard_map/ppermute | solution.py:382
  969.5 14.3 %collective-permute-start.29 = (bf16[2,64,1024]{2,1,0:T(8,128)(2,1)S(1)}, bf16[2,64,1024]{2,1,0:T(8,128)(2,1)S(1)}, u32[]{:S(2)}, u32[]{:S(2)}) collective-permute-start(bf16[2,64,1024]{2,1,0:T(8,128)(2,1)S(1)} %collective-permute-done.28), channel_id=1, source_target_pairs={{0,1},{1,0},{2,3},{3,2},{4,5},{5,4},{6,7},{7,6},{8,9},{9,8},{10,11... | collective-permute-start | bytes 786440 | tf_op jit(solution)/shard_map/ppermute | solution.py:382
  983.9 12.0 %collective-permute-start.14 = (bf16[2,128,1024]{2,1,0:T(8,128)(2,1)}, bf16[2,128,1024]{2,1,0:T(8,128)(2,1)S(1)}, u32[]{:S(2)}, u32[]{:S(2)}) collective-permute-start(bf16[2,128,1024]{2,1,0:T(8,128)(2,1)} %collective-permute-done.13), channel_id=1, source_target_pairs={{0,1},{1,0},{2,3},{3,2},{4,5},{5,4},{6,7},{7,6},{8,9},{9,8},{10,11... | collective-permute-start | bytes 1572872 | tf_op jit(solution)/shard_map/ppermute | solution.py:381
  988.1 11.9 %collective-permute-start.23 = (bf16[2,128,1024]{2,1,0:T(8,128)(2,1)}, bf16[2,128,1024]{2,1,0:T(8,128)(2,1)S(1)}, u32[]{:S(2)}, u32[]{:S(2)}) collective-permute-start(bf16[2,128,1024]{2,1,0:T(8,128)(2,1)} %collective-permute-done.22), channel_id=1, source_target_pairs={{0,1},{1,0},{2,3},{3,2},{4,5},{5,4},{6,7},{7,6},{8,9},{9,8},{10,11... | collective-permute-start | bytes 1572872 | tf_op jit(solution)/shard_map/ppermute | solution.py:381
  991.2 50.2 %collective-permute-start.40 = (bf16[2,128,4096]{2,1,0:T(8,128)(2,1)S(1)}, bf16[2,128,4096]{2,1,0:T(8,128)(2,1)S(1)}, u32[]{:S(2)}, u32[]{:S(2)}) collective-permute-start(bf16[2,128,4096]{2,1,0:T(8,128)(2,1)S(1)} %get-tuple-element.133), channel_id=1, source_target_pairs={{0,2},{1,3},{2,4},{3,5},{4,6},{5,7},{6,0},{7,1},{8,10},{9,11},{10,... | collective-permute-start | bytes 6291464 | tf_op jit(solution)/shard_map/ppermute | solution.py:375
  992.2 93.5 %collective-permute-start.49 = (bf16[2,512,1024]{2,1,0:T(8,128)(2,1)S(1)}, bf16[2,512,1024]{2,1,0:T(8,128)(2,1)S(1)}, u32[]{:S(2)}, u32[]{:S(2)}) collective-permute-start(bf16[2,512,1024]{2,1,0:T(8,128)(2,1)S(1)} %get-tuple-element.131), channel_id=1, source_target_pairs={{0,2},{1,3},{2,4},{3,5},{4,6},{5,7},{6,0},{7,1},{8,10},{9,11},{10,... | collective-permute-start | bytes 6291464 | tf_op jit(solution)/shard_map/ppermute | solution.py:375
  998.5 90.2 %collective-permute-start.51 = (bf16[2,512,1024]{2,1,0:T(8,128)(2,1)S(1)}, bf16[2,512,1024]{2,1,0:T(8,128)(2,1)S(1)}, u32[]{:S(2)}, u32[]{:S(2)}) collective-permute-start(bf16[2,512,1024]{2,1,0:T(8,128)(2,1)S(1)} %get-tuple-element.131), channel_id=1, source_target_pairs={{0,6},{1,7},{2,0},{3,1},{4,2},{5,3},{6,4},{7,5},{8,14},{9,15},{10,... | collective-permute-start | bytes 6291464 | tf_op jit(solution)/shard_map/ppermute | solution.py:376
  1005.7 87.4 %collective-permute-start.39 = (bf16[2,128,4096]{2,1,0:T(8,128)(2,1)S(1)}, bf16[2,128,4096]{2,1,0:T(8,128)(2,1)S(1)}, u32[]{:S(2)}, u32[]{:S(2)}) collective-permute-start(bf16[2,128,4096]{2,1,0:T(8,128)(2,1)S(1)} %get-tuple-element.133), channel_id=1, source_target_pairs={{0,1},{1,0},{2,3},{3,2},{4,5},{5,4},{6,7},{7,6},{8,9},{9,8},{10,11... | collective-permute-start | bytes 6291464 | tf_op jit(solution)/shard_map/ppermute | solution.py:381
  1008.2 87.2 %collective-permute-start.42 = (bf16[2,128,4096]{2,1,0:T(8,128)(2,1)S(1)}, bf16[2,128,4096]{2,1,0:T(8,128)(2,1)S(1)}, u32[]{:S(2)}, u32[]{:S(2)}) collective-permute-start(bf16[2,128,4096]{2,1,0:T(8,128)(2,1)S(1)} %get-tuple-element.133), channel_id=1, source_target_pairs={{0,6},{1,7},{2,0},{3,1},{4,2},{5,3},{6,4},{7,5},{8,14},{9,15},{10,... | collective-permute-start | bytes 6291464 | tf_op jit(solution)/shard_map/ppermute | solution.py:376
  1041.4 57.2 %collective-permute-start.48 = (bf16[2,512,1024]{2,1,0:T(8,128)(2,1)S(1)}, bf16[2,512,1024]{2,1,0:T(8,128)(2,1)S(1)}, u32[]{:S(2)}, u32[]{:S(2)}) collective-permute-start(bf16[2,512,1024]{2,1,0:T(8,128)(2,1)S(1)} %get-tuple-element.131), channel_id=1, source_target_pairs={{0,1},{1,0},{2,3},{3,2},{4,5},{5,4},{6,7},{7,6},{8,9},{9,8},{10,11... | collective-permute-start | bytes 6291464 | tf_op jit(solution)/shard_map/ppermute | solution.py:381
  1085.7 33.8 %collective-permute-start.50 = (bf16[2,512,1024]{2,1,0:T(8,128)(2,1)S(1)}, bf16[2,512,1024]{2,1,0:T(8,128)(2,1)S(1)}, u32[]{:S(2)}, u32[]{:S(2)}) collective-permute-start(bf16[2,512,1024]{2,1,0:T(8,128)(2,1)S(1)} %collective-permute-done.49), channel_id=1, source_target_pairs={{0,1},{1,0},{2,3},{3,2},{4,5},{5,4},{6,7},{7,6},{8,9},{9,8},{10,11... | collective-permute-start | bytes 6291464 | tf_op jit(solution)/shard_map/ppermute | solution.py:381
  1088.7 35.5 %collective-permute-start.52 = (bf16[2,512,1024]{2,1,0:T(8,128)(2,1)S(1)}, bf16[2,512,1024]{2,1,0:T(8,128)(2,1)S(1)}, u32[]{:S(2)}, u32[]{:S(2)}) collective-permute-start(bf16[2,512,1024]{2,1,0:T(8,128)(2,1)S(1)} %collective-permute-done.51), channel_id=1, source_target_pairs={{0,1},{1,0},{2,3},{3,2},{4,5},{5,4},{6,7},{7,6},{8,9},{9,8},{10,11... | collective-permute-start | bytes 6291464 | tf_op jit(solution)/shard_map/ppermute | solution.py:381
  1093.1 26.4 %collective-permute-start.44 = (bf16[2,64,4096]{2,1,0:T(8,128)(2,1)S(1)}, bf16[2,64,4096]{2,1,0:T(8,128)(2,1)S(1)}, u32[]{:S(2)}, u32[]{:S(2)}) collective-permute-start(bf16[2,64,4096]{2,1,0:T(8,128)(2,1)S(1)} %slice.436), channel_id=1, source_target_pairs={{0,2},{1,3},{2,4},{3,5},{4,6},{5,7},{6,0},{7,1},{8,10},{9,11},{10,... | collective-permute-start | bytes 3145736 | tf_op jit(solution)/shard_map/ppermute | solution.py:377
  1095.4 51.9 %collective-permute-start.41 = (bf16[2,128,4096]{2,1,0:T(8,128)(2,1)S(1)}, bf16[2,128,4096]{2,1,0:T(8,128)(2,1)S(1)}, u32[]{:S(2)}, u32[]{:S(2)}) collective-permute-start(bf16[2,128,4096]{2,1,0:T(8,128)(2,1)S(1)} %collective-permute-done.40), channel_id=1, source_target_pairs={{0,1},{1,0},{2,3},{3,2},{4,5},{5,4},{6,7},{7,6},{8,9},{9,8},{10,11... | collective-permute-start | bytes 6291464 | tf_op jit(solution)/shard_map/ppermute | solution.py:381
  1098.6 46.5 %collective-permute-start.46 = (bf16[2,64,4096]{2,1,0:T(8,128)(2,1)S(1)}, bf16[2,64,4096]{2,1,0:T(8,128)(2,1)S(1)}, u32[]{:S(2)}, u32[]{:S(2)}) collective-permute-start(bf16[2,64,4096]{2,1,0:T(8,128)(2,1)S(1)} %slice.437), channel_id=1, source_target_pairs={{0,6},{1,7},{2,0},{3,1},{4,2},{5,3},{6,4},{7,5},{8,14},{9,15},{10,... | collective-permute-start | bytes 3145736 | tf_op jit(solution)/shard_map/ppermute | solution.py:378
  1119.5 25.4 %collective-permute-start.53 = (bf16[2,256,1024]{2,1,0:T(8,128)(2,1)S(1)}, bf16[2,256,1024]{2,1,0:T(8,128)(2,1)S(1)}, u32[]{:S(2)}, u32[]{:S(2)}) collective-permute-start(bf16[2,256,1024]{2,1,0:T(8,128)(2,1)S(1)} %slice.438), channel_id=1, source_target_pairs={{0,2},{1,3},{2,4},{3,5},{4,6},{5,7},{6,0},{7,1},{8,10},{9,11},{10,... | collective-permute-start | bytes 3145736 | tf_op jit(solution)/shard_map/ppermute | solution.py:377
  1119.5 27.8 %collective-permute-start.55 = (bf16[2,256,1024]{2,1,0:T(8,128)(2,1)S(1)}, bf16[2,256,1024]{2,1,0:T(8,128)(2,1)S(1)}, u32[]{:S(2)}, u32[]{:S(2)}) collective-permute-start(bf16[2,256,1024]{2,1,0:T(8,128)(2,1)S(1)} %slice.439), channel_id=1, source_target_pairs={{0,6},{1,7},{2,0},{3,1},{4,2},{5,3},{6,4},{7,5},{8,14},{9,15},{10,... | collective-permute-start | bytes 3145736 | tf_op jit(solution)/shard_map/ppermute | solution.py:378
  1124.2 26.6 %collective-permute-start.43 = (bf16[2,128,4096]{2,1,0:T(8,128)(2,1)S(1)}, bf16[2,128,4096]{2,1,0:T(8,128)(2,1)S(1)}, u32[]{:S(2)}, u32[]{:S(2)}) collective-permute-start(bf16[2,128,4096]{2,1,0:T(8,128)(2,1)S(1)} %collective-permute-done.42), channel_id=1, source_target_pairs={{0,1},{1,0},{2,3},{3,2},{4,5},{5,4},{6,7},{7,6},{8,9},{9,8},{10,11... | collective-permute-start | bytes 6291464 | tf_op jit(solution)/shard_map/ppermute | solution.py:381
  (214 other events, 1899.7 us)
Sparse Core Ops, SparseCore 0:
  13.6 39.6 all-gather.11
  55.4 44.0 all-gather.13
  173.9 38.2 all-gather.9
  214.2 44.2 all-gather.7
  337.5 103.9 reduce-scatter.6
  444.3 137.8 reduce-scatter.8
  587.8 33.4 reduce-scatter.10
  623.6 92.1 reduce-scatter.12
  718.7 126.7 reduce-scatter.14
  848.1 42.2 reduce-scatter.16
